TPU v7x, 32 devices: a whole 2x2x4 slice. The times are simulated.
32 devices in a mesh: row: 8 (over y, x, core), col: 4 (over z).
Axes of the slice: x: 2, y: 2, z: 4, core: 2. Of those that a mesh axis runs over, the one named last changes fastest.
Arguments:
- residual: float32 [2048, 2048], P('row', 'col'), may hold values from -0.15625 to 0.15625
- direction: float32 [2048, 2048], P('row', 'col'), may hold values from -6 to 6
- ground_shift: float32 [1], replicated, may hold values from 1.6937256e-06 to 6.7749024e-06
- previous: float32 [1], replicated, may hold values from 192 to 768
Outputs:
- next_direction: float32 [2048, 2048], P('row', 'col')
- step_ratio: float32 [1], replicated
All inputs are finite; a program needn't handle non-finite values.
Results may differ from a plain program's by a relative error of at most 0.00015.
Values sent between devices are 32-bit elements; how exact they have to be, the bound alone decides.
A program may use at most 64 MiB of HBM per device.

v0:
```python
import functools
import math

import jax
import jax.numpy as jnp
import numpy as np
from jax import lax
from jax.experimental import pallas as pl
from jax.experimental.pallas import tpu as pltpu
from jax.sharding import PartitionSpec as P

MESH = pl.DeviceIdType.MESH


def base_tables(extent, devices):
    length = extent * devices
    half = extent // 2
    odd = 2 * np.arange(extent, dtype=np.int64)[:, None] + 1
    steps = 2 * devices * np.arange(half + 1, dtype=np.int64)[None, :]
    coarse = np.pi * (steps * odd % (4 * length)) / (2 * length)
    scale = math.sqrt(2.0 / length)
    cos_a, sin_a = scale * np.cos(coarse), scale * np.sin(coarse)
    lanes = -(-(devices + 1) // 128) * 128
    fine = np.pi * np.arange(lanes, dtype=np.int64)[None, :] * odd / (2 * length)
    coarse_tables = np.stack([cos_a[:, :-1], sin_a[:, :-1], cos_a[:, 1:], sin_a[:, 1:]])
    fine_tables = np.stack([np.cos(fine), np.sin(fine)])
    waves = []
    for t in range(devices):
        second = devices if t == 0 else 2 * devices - t
        waves.append(2 * devices * np.arange(half) + t)
        waves.append(2 * devices * np.arange(half) + second)
    waves = np.concatenate(waves)
    eigen = 4.0 * np.sin(np.pi * waves / (2 * length)) ** 2
    return (
        coarse_tables.astype(np.float32),
        fine_tables.astype(np.float32),
        eigen.astype(np.float32)[None, :],
    )


def mixing(devices):
    target = np.arange(devices)[:, None]
    source = np.arange(devices)[None, :]
    angles = np.pi * (target * source % (2 * devices)) / devices
    parity = np.where(source % 2 == 0, 1.0, -1.0)
    return np.cos(angles), np.where(target > 0, np.sin(angles), parity)


def weighted_sum(coefs, terms):
    total = None
    for coef, term in zip(coefs, terms):
        coef = float(coef)
        if abs(coef) < 1e-12:
            continue
        if abs(coef - 1.0) < 1e-12:
            total = term if total is None else total + term
        elif abs(coef + 1.0) < 1e-12:
            total = -term if total is None else total - term
        else:
            total = coef * term if total is None else total + coef * term
    return total


def split(value):
    high = value.astype(jnp.bfloat16)
    return high, (value - high.astype(jnp.float32)).astype(jnp.bfloat16)


def kernel(
    rows,
    cols,
    residual_hbm,
    direction_hbm,
    coarse_hbm,
    fine_hbm,
    eigen_ref,
    shift_ref,
    previous_ref,
    out_hbm,
    ratio_ref,
    residual_ref,
    direction_ref,
    coarse_ref,
    fine_ref,
    out_ref,
    load_sems,
    store_sems,
    out1,
    in1,
    out2,
    in2,
    table_hi,
    table_lo,
    field,
    from_left,
    from_right,
    own_hi,
    own_lo,
    carried_hi,
    carried_lo,
    added,
    rowsum,
    colsum,
    carry,
    s1,
    r1,
    s2,
    r2,
    s3,
    r3,
    s5,
    r5,
):
    me_r = lax.axis_index("row")
    me_c = lax.axis_index("col")
    extent = residual_ref.shape[0]
    width = out1.shape[1]
    half = extent // 2
    total_cols = width * rows * cols
    f32 = jnp.float32
    mix_cos, mix_sin = mixing(rows)

    barrier = pltpu.get_barrier_semaphore()
    for o in range(1, rows):
        pl.semaphore_signal(
            barrier, inc=1, device_id={"row": lax.rem(me_r + o, rows)}, device_id_type=MESH
        )
    for o in range(1, cols):
        pl.semaphore_signal(
            barrier, inc=1, device_id={"col": lax.rem(me_c + o, cols)}, device_id_type=MESH
        )

    loads = []
    for i, (source, landing) in enumerate(
        (
            (residual_hbm, residual_ref),
            (coarse_hbm, coarse_ref),
            (fine_hbm, fine_ref),
            (direction_hbm, direction_ref),
        )
    ):
        copy = pltpu.make_async_copy(source, landing, load_sems.at[i])
        copy.start()
        loads.append(copy)

    def share(axis, me, count, source, landing, send_sems, recv_sems):
        copies = []
        for o in range(1, count):
            to = lax.rem(me + o, count)
            copy = pltpu.make_async_remote_copy(
                src_ref=source(to),
                dst_ref=landing.at[me],
                send_sem=send_sems.at[o - 1],
                recv_sem=recv_sems.at[o - 1],
                device_id={axis: to},
                device_id_type=MESH,
            )
            copy.start()
            copies.append(copy)
        return copies

    loads[0].wait()
    for e in range(0, residual_ref.shape[1], 128):
        turned = residual_ref[:, e : e + 128].T
        for i in range(128 // width):
            out1[e // width + i] = turned[i * width : (i + 1) * width]
    pl.semaphore_wait(barrier, rows + cols - 2)
    first = share("row", me_r, rows, lambda to: out1.at[to], in1, s1, r1)
    in1[me_r] = out1[me_r]

    loads[1].wait()
    loads[2].wait()

    def quadrants(t):
        if t == 0:
            lane = lax.broadcasted_iota(jnp.int32, (extent, half), 1)
            one = jnp.where(lane == 0, math.sqrt(0.5), 1.0) * coarse_ref[0]
            cos_b = fine_ref[0, :, rows : rows + 1]
            sin_b = fine_ref[1, :, rows : rows + 1]
            two = coarse_ref[0] * cos_b - coarse_ref[1] * sin_b
            zero = jnp.zeros_like(one)
            return ((one, zero), (zero, two))
        cos_b = fine_ref[0, :, t : t + 1]
        sin_b = fine_ref[1, :, t : t + 1]
        return (
            (
                coarse_ref[0] * cos_b - coarse_ref[1] * sin_b,
                coarse_ref[2] * cos_b + coarse_ref[3] * sin_b,
            ),
            (
                -(coarse_ref[1] * cos_b + coarse_ref[0] * sin_b),
                coarse_ref[3] * cos_b - coarse_ref[2] * sin_b,
            ),
        )

    for t in range(rows):
        quads = quadrants(t)
        for i in range(2):
            for j in range(2):
                high, low = split(quads[i][j])
                at = (t, slice(i * extent, (i + 1) * extent), slice(j * half, (j + 1) * half))
                table_hi[at] = high
                table_lo[at] = low

    alpha = eigen_ref[...] + shift_ref[...]
    h = 0.5 * jnp.sqrt(alpha)
    z = h / (1.0 + jnp.sqrt(1.0 + h * h))
    z2 = z * z
    series = jnp.full_like(z, 1.0 / 23)
    for p in range(21, 0, -2):
        series = series * z2 + 1.0 / p
    theta = 4.0 * z * series
    gain = 0.5 / jnp.sqrt(alpha * (1.0 + 0.25 * alpha))

    q_one = jnp.exp(-theta)
    place = lax.broadcasted_iota(jnp.int32, (width, extent), 0)
    fplace = place.astype(f32)
    for t in range(rows):
        lanes = slice(t * extent, (t + 1) * extent)
        from_left[:, lanes] = gain[:, lanes] * jnp.exp(-theta[:, lanes] * (fplace + 1.0))
        from_right[:, lanes] = gain[:, lanes] * jnp.exp(-theta[:, lanes] * (width - fplace))
    chunk = jnp.exp(-theta * float(width))
    group = jnp.exp(-theta * float(width * rows))
    whole = jnp.exp(-theta * float(total_cols))

    for copy in first:
        copy.wait_recv()

    length = rows * extent
    partial = jnp.zeros((1, extent), f32)
    for t in range(rows):
        lanes = slice(t * extent, (t + 1) * extent)
        pieces = [in1[d] for d in range(rows)]
        real = weighted_sum(mix_cos[t], pieces)
        imag = weighted_sum(mix_sin[t], pieces)
        high, low = split(jnp.concatenate([real, imag], axis=1))
        both = jnp.dot(
            jnp.concatenate([high, low], axis=0), table_hi[t], preferred_element_type=f32
        )
        value = (
            both[:width] + both[width:] + jnp.dot(high, table_lo[t], preferred_element_type=f32)
        )
        ahead = value
        behind = value
        q = q_one[:, lanes]
        s = 1
        while s < width:
            ahead = ahead + q * jnp.where(place >= s, pltpu.roll(ahead, s, 0), 0.0)
            behind = behind + q * jnp.where(
                place < width - s, pltpu.roll(behind, width - s, 0), 0.0
            )
            q = q * q
            s *= 2
        solved = gain[:, lanes] * (ahead + behind - value)
        partial = partial + jnp.sum(value * solved, axis=0, keepdims=True)
        field[:, lanes] = solved
        rowsum[me_r, 0:1, lanes] = ahead[width - 1 : width]
        rowsum[me_r, 1:2, lanes] = behind[0:1]

    def fold(row):
        return sum(row[:, i : i + 128] for i in range(0, row.shape[1], 128))

    spare = slice(length, length + 128)
    rowsum[me_r, 0:1, spare] = fold(partial)
    rowsum[me_r, 1:2, spare] = jnp.zeros((1, 128), f32)
    mine = rowsum.at[me_r]
    second = share("row", me_r, rows, lambda to: mine, rowsum, s2, r2)

    turn = (((1,), (1,)), ((), ()))
    reals, imags = [], []
    for t in range(rows):
        lanes = slice(t * extent, (t + 1) * extent)
        high, low = split(field[:, lanes])
        both = lax.dot_general(
            jnp.concatenate([high, low], axis=0), table_hi[t], turn, preferred_element_type=f32
        )
        value = (
            both[:width]
            + both[width:]
            + lax.dot_general(high, table_lo[t], turn, preferred_element_type=f32)
        )
        reals.append(value[:, :extent])
        imags.append(value[:, extent:])
    for d in range(rows):
        out2[d] = weighted_sum(list(mix_cos[:, d]) + list(mix_sin[:, d]), reals + imags)
    fifth = share("row", me_r, rows, lambda to: out2.at[to], in2, s5, r5)
    in2[me_r] = out2[me_r]
    for copy in second:
        copy.wait_recv()

    def carries(sums, count, ratio):
        left, right = [jnp.zeros_like(ratio)], [jnp.zeros_like(ratio)]
        for k in range(count):
            left.append(ratio * left[-1] + sums[k, 0:1, :length])
            right.append(ratio * right[-1] + sums[count - 1 - k, 1:2, :length])
        return left[:-1], right[count - 1 :: -1], left[-1], right[-1]

    weight = gain * q_one
    lefts, rights, at_end, at_start = carries(rowsum, rows, chunk)
    coupled = jnp.zeros_like(weight)
    inner = jnp.zeros((1, 128), f32)
    for k in range(rows):
        carry[k, 0:1, :] = lefts[k]
        carry[k, 1:2, :] = rights[k]
        coupled = coupled + lefts[k] * rowsum[k, 1:2, :length] + rights[k] * rowsum[k, 0:1, :length]
        inner = inner + rowsum[k, 0:1, spare]
    colsum[me_c, 0:1, :length] = at_end
    colsum[me_c, 1:2, :length] = at_start
    colsum[me_c, 0:1, spare] = inner + fold(weight * coupled)
    colsum[me_c, 1:2, spare] = jnp.zeros((1, 128), f32)
    mine_c = colsum.at[me_c]
    third = share("col", me_c, cols, lambda to: mine_c, colsum, s3, r3)

    for t in range(rows):
        quads = quadrants(t)
        cos_d, sin_d = f32(mix_cos[t, 0]), f32(mix_sin[t, 0])
        for d in range(1, rows):
            cos_d = jnp.where(me_r == d, f32(mix_cos[t, d]), cos_d)
            sin_d = jnp.where(me_r == d, f32(mix_sin[t, d]), sin_d)
        for j in range(2):
            high, low = split(cos_d * quads[0][j] + sin_d * quads[1][j])
            lanes = slice(t * extent + j * half, t * extent + (j + 1) * half)
            own_hi[:, lanes] = high
            own_lo[:, lanes] = low
    for copy in third:
        copy.wait_recv()

    lefts, rights, at_end, at_start = carries(colsum, cols, group)
    images = 1.0 / (1.0 - whole * whole)
    entry = (at_start + whole * at_end) * images
    exit_ = (at_end + whole * at_start) * images
    for k in range(cols):
        lefts[k] = lefts[k] + entry
        rights[cols - 1 - k] = rights[cols - 1 - k] + exit_
        entry, exit_ = entry * group, exit_ * group
    coupled = jnp.zeros_like(weight)
    inner = jnp.zeros((1, 128), f32)
    left_c, right_c = lefts[0], rights[0]
    for k in range(cols):
        left_c = jnp.where(me_c == k, lefts[k], left_c)
        right_c = jnp.where(me_c == k, rights[k], right_c)
        coupled = coupled + lefts[k] * colsum[k, 1:2, :length] + rights[k] * colsum[k, 0:1, :length]
        inner = inner + colsum[k, 0:1, spare]
    inner = jnp.sum(inner + fold(weight * coupled), axis=1, keepdims=True)
    ratio = inner / previous_ref[...]
    ratio_ref[...] = jnp.broadcast_to(ratio, ratio_ref.shape)
    for k in range(rows):
        carry[k, 0:1, :] = carry[k, 0:1, :] + left_c
        carry[rows - 1 - k, 1:2, :] = carry[rows - 1 - k, 1:2, :] + right_c
        left_c, right_c = left_c * chunk, right_c * chunk

    per = 128 // width
    block = out_ref.shape[1]
    for e in range(0, out_ref.shape[1], block):
        for r in range(e // width, (e + block) // width):
            at = slice(r * width, (r + 1) * width)
            for t in range(rows):
                lanes = slice(t * extent, (t + 1) * extent)
                high, low = split(
                    from_left[:, lanes] * carry[r, 0:1, lanes]
                    + from_right[:, lanes] * carry[r, 1:2, lanes]
                )
                carried_hi[at, lanes] = high
                carried_lo[at, lanes] = low
        at = slice(e, e + block)
        added[at, :] = (
            lax.dot_general(carried_hi[at, :], own_hi[...], turn, preferred_element_type=f32)
            + lax.dot_general(carried_lo[at, :], own_hi[...], turn, preferred_element_type=f32)
            + lax.dot_general(carried_hi[at, :], own_lo[...], turn, preferred_element_type=f32)
        )
    for copy in fifth:
        copy.wait_recv()
    loads[3].wait()
    stores = []
    for e in range(0, out_ref.shape[1], 128):
        turned = jnp.concatenate([in2[e // width + i] for i in range(per)], axis=0)
        turned = turned + added[e : e + 128, :]
        out_ref[:, e : e + 128] = turned.T + ratio * direction_ref[:, e : e + 128]
        copy = pltpu.make_async_copy(
            out_ref.at[:, e : e + 128], out_hbm.at[:, e : e + 128], store_sems.at[e // 128]
        )
        copy.start()
        stores.append(copy)
    for copy in stores:
        copy.wait()
    for copies in (first, second, third, fifth):
        for copy in copies:
            copy.wait_send()


def body(rows, cols, residual, direction, ground_shift, previous):
    extent, here = residual.shape
    width = here // rows
    length = extent * rows
    f32 = jnp.float32
    coarse, fine, eigen = base_tables(extent, rows)
    vmem = pl.BlockSpec(memory_space=pltpu.VMEM)
    smem = pl.BlockSpec(memory_space=pltpu.SMEM)
    dma = pltpu.SemaphoreType.DMA
    per_row, per_col = max(rows - 1, 1), max(cols - 1, 1)
    anywhere = pl.BlockSpec(memory_space=pl.ANY)
    output, ratio = pl.pallas_call(
        functools.partial(kernel, rows, cols),
        out_shape=(
            jax.ShapeDtypeStruct((extent, here), f32),
            jax.ShapeDtypeStruct((1, 1), f32),
        ),
        in_specs=[anywhere, anywhere, anywhere, anywhere, vmem, vmem, vmem],
        out_specs=(anywhere, vmem),
        scratch_shapes=[
            pltpu.VMEM((extent, here), f32),
            pltpu.VMEM((extent, here), f32),
            pltpu.VMEM(coarse.shape, f32),
            pltpu.VMEM(fine.shape, f32),
            pltpu.VMEM((extent, here), f32),
            dma((4,)),
            dma((here // 128,)),
            pltpu.VMEM((rows, width, extent), f32),
            pltpu.VMEM((rows, width, extent), f32),
            pltpu.VMEM((rows, width, extent), f32),
            pltpu.VMEM((rows, width, extent), f32),
            pltpu.VMEM((rows, 2 * extent, extent), jnp.bfloat16),
            pltpu.VMEM((rows, 2 * extent, extent), jnp.bfloat16),
            pltpu.VMEM((width, length), f32),
            pltpu.VMEM((width, length), f32),
            pltpu.VMEM((width, length), f32),
            pltpu.VMEM((extent, length), jnp.bfloat16),
            pltpu.VMEM((extent, length), jnp.bfloat16),
            pltpu.VMEM((here, length), jnp.bfloat16),
            pltpu.VMEM((here, length), jnp.bfloat16),
            pltpu.VMEM((here, extent), f32),
            pltpu.VMEM((rows, 2, length + 128), f32),
            pltpu.VMEM((cols, 2, length + 128), f32),
            pltpu.VMEM((rows, 2, length), f32),
            dma((per_row,)),
            dma((per_row,)),
            dma((per_row,)),
            dma((per_row,)),
            dma((per_col,)),
            dma((per_col,)),
            dma((per_row,)),
            dma((per_row,)),
        ],
        compiler_params=pltpu.CompilerParams(collective_id=0, has_side_effects=True),
    )(residual, direction, coarse, fine, eigen, ground_shift.reshape(1, 1), previous.reshape(1, 1))
    return output, ratio.reshape(1)


def solution(mesh):
    return jax.shard_map(
        functools.partial(body, mesh.shape["row"], mesh.shape["col"]),
        mesh=mesh,
        in_specs=(P("row", "col"), P("row", "col"), P(), P()),
        out_specs=(P("row", "col"), P()),
        check_vma=False,
    )
```

profile of v0, /device:TPU:0, one launch (start us, length us, event | category | flops | bytes accessed | tf_op | source)
XLA Modules:
  0.0 31.9 jit_solution(7042743739212868865)
XLA Ops:
  1.9 26.4 %shard_map.86 = (f32[256,512]{1,0:T(8,128)}, f32[1,1]{1,0:T(1,128)}) custom-call(f32[256,512]{1,0:T(8,128)} %residual_hbm.1, f32[256,512]{1,0:T(8,128)} %direction_hbm.1, f32[4,256,128]{2,1,0:T(8,128)} %constant.6.clone.coarse_hbm, f32[2,256,128]{2,1,0:T(8,128)} %constant.7.clone.fine_hbm, f32[1,2048]{1,0:T(1,128)} %constant.8.clone.eigen_ref, ...), custom_call_target="tpu_custom_call" | custom-call | tf_op jit(solution)/shard_map/pallas_call | solution.py:402
  28.3 1.9 %copy.13 = f32[256,512]{1,0:T(8,128)} copy(f32[256,512]{1,0:T(8,128)} %get-tuple-element.8) | data formatting | bytes 1048576
where the time goes:
time: 32.1 us; the launch traced here: 31.9 us
  Pallas kernels  26.4 us (82%)
  between operations  3.63 us (11%)
  local copies, waits for them, and re-layouts  1.87 us (6%)
    pallas_call x1, Pallas kernels, body(): pl.pallas_call(functools.partial(kernel, rows, cols), out_shape=(jax.Shap...  26.4 us
    unnamed x1, local copies, waits for them, and re-layouts  1.87 us

commit v1 on v0

--- a/solution.py
+++ b/solution.py
@@ -70,21 +70,20 @@
     rows,
     cols,
     residual_hbm,
-    direction_hbm,
     coarse_hbm,
     fine_hbm,
+    eigen_hbm,
+    shift_hbm,
+    previous_hbm,
+    out_ref,
+    ratio_ref,
+    residual_ref,
+    coarse_ref,
+    fine_ref,
     eigen_ref,
     shift_ref,
     previous_ref,
-    out_hbm,
-    ratio_ref,
-    residual_ref,
-    direction_ref,
-    coarse_ref,
-    fine_ref,
-    out_ref,
     load_sems,
-    store_sems,
     out1,
     in1,
     out2,
@@ -136,7 +135,9 @@
             (residual_hbm, residual_ref),
             (coarse_hbm, coarse_ref),
             (fine_hbm, fine_ref),
-            (direction_hbm, direction_ref),
+            (eigen_hbm, eigen_ref),
+            (shift_hbm, shift_ref),
+            (previous_hbm, previous_ref),
         )
     ):
         copy = pltpu.make_async_copy(source, landing, load_sems.at[i])
@@ -202,7 +203,9 @@
                 table_hi[at] = high
                 table_lo[at] = low
 
-    alpha = eigen_ref[...] + shift_ref[...]
+    for copy in loads[3:]:
+        copy.wait()
+    alpha = eigen_ref[...] + shift_ref[0]
     h = 0.5 * jnp.sqrt(alpha)
     z = h / (1.0 + jnp.sqrt(1.0 + h * h))
     z2 = z * z
@@ -342,7 +345,7 @@
         coupled = coupled + lefts[k] * colsum[k, 1:2, :length] + rights[k] * colsum[k, 0:1, :length]
         inner = inner + colsum[k, 0:1, spare]
     inner = jnp.sum(inner + fold(weight * coupled), axis=1, keepdims=True)
-    ratio = inner / previous_ref[...]
+    ratio = inner / previous_ref[0]
     ratio_ref[...] = jnp.broadcast_to(ratio, ratio_ref.shape)
     for k in range(rows):
         carry[k, 0:1, :] = carry[k, 0:1, :] + left_c
@@ -370,19 +373,10 @@
         )
     for copy in fifth:
         copy.wait_recv()
-    loads[3].wait()
-    stores = []
     for e in range(0, out_ref.shape[1], 128):
         turned = jnp.concatenate([in2[e // width + i] for i in range(per)], axis=0)
         turned = turned + added[e : e + 128, :]
-        out_ref[:, e : e + 128] = turned.T + ratio * direction_ref[:, e : e + 128]
-        copy = pltpu.make_async_copy(
-            out_ref.at[:, e : e + 128], out_hbm.at[:, e : e + 128], store_sems.at[e // 128]
-        )
-        copy.start()
-        stores.append(copy)
-    for copy in stores:
-        copy.wait()
+        out_ref[:, e : e + 128] = turned.T
     for copies in (first, second, third, fifth):
         for copy in copies:
             copy.wait_send()
@@ -398,52 +392,75 @@
     smem = pl.BlockSpec(memory_space=pltpu.SMEM)
     dma = pltpu.SemaphoreType.DMA
     per_row, per_col = max(rows - 1, 1), max(cols - 1, 1)
-    anywhere = pl.BlockSpec(memory_space=pl.ANY)
-    output, ratio = pl.pallas_call(
+    hbm = pl.BlockSpec(memory_space=pltpu.HBM)
+    scratch = [
+        pltpu.VMEM((extent, here), f32),
+        pltpu.VMEM(coarse.shape, f32),
+        pltpu.VMEM(fine.shape, f32),
+        pltpu.VMEM(eigen.shape, f32),
+        pltpu.SMEM((1,), f32),
+        pltpu.SMEM((1,), f32),
+        dma((6,)),
+        pltpu.VMEM((rows, width, extent), f32),
+        pltpu.VMEM((rows, width, extent), f32),
+        pltpu.VMEM((rows, width, extent), f32),
+        pltpu.VMEM((rows, width, extent), f32),
+        pltpu.VMEM((rows, 2 * extent, extent), jnp.bfloat16),
+        pltpu.VMEM((rows, 2 * extent, extent), jnp.bfloat16),
+        pltpu.VMEM((width, length), f32),
+        pltpu.VMEM((width, length), f32),
+        pltpu.VMEM((width, length), f32),
+        pltpu.VMEM((extent, length), jnp.bfloat16),
+        pltpu.VMEM((extent, length), jnp.bfloat16),
+        pltpu.VMEM((here, length), jnp.bfloat16),
+        pltpu.VMEM((here, length), jnp.bfloat16),
+        pltpu.VMEM((here, extent), f32),
+        pltpu.VMEM((rows, 2, length + 128), f32),
+        pltpu.VMEM((cols, 2, length + 128), f32),
+        pltpu.VMEM((rows, 2, length), f32),
+        dma((per_row,)),
+        dma((per_row,)),
+        dma((per_row,)),
+        dma((per_row,)),
+        dma((per_col,)),
+        dma((per_col,)),
+        dma((per_row,)),
+        dma((per_row,)),
+    ]
+    held = sum(
+        math.prod(ref.shape) * jnp.dtype(ref.dtype).itemsize
+        for ref in scratch
+        if ref.memory_space == pltpu.VMEM
+    )
+    solved, ratio = pl.pallas_call(
         functools.partial(kernel, rows, cols),
         out_shape=(
             jax.ShapeDtypeStruct((extent, here), f32),
-            jax.ShapeDtypeStruct((1, 1), f32),
+            jax.ShapeDtypeStruct((1, 128), f32),
         ),
-        in_specs=[anywhere, anywhere, anywhere, anywhere, vmem, vmem, vmem],
-        out_specs=(anywhere, vmem),
-        scratch_shapes=[
-            pltpu.VMEM((extent, here), f32),
-            pltpu.VMEM((extent, here), f32),
-            pltpu.VMEM(coarse.shape, f32),
-            pltpu.VMEM(fine.shape, f32),
-            pltpu.VMEM((extent, here), f32),
-            dma((4,)),
-            dma((here // 128,)),
-            pltpu.VMEM((rows, width, extent), f32),
-            pltpu.VMEM((rows, width, extent), f32),
-            pltpu.VMEM((rows, width, extent), f32),
-            pltpu.VMEM((rows, width, extent), f32),
-            pltpu.VMEM((rows, 2 * extent, extent), jnp.bfloat16),
-            pltpu.VMEM((rows, 2 * extent, extent), jnp.bfloat16),
-            pltpu.VMEM((width, length), f32),
-            pltpu.VMEM((width, length), f32),
-            pltpu.VMEM((width, length), f32),
-            pltpu.VMEM((extent, length), jnp.bfloat16),
-            pltpu.VMEM((extent, length), jnp.bfloat16),
-            pltpu.VMEM((here, length), jnp.bfloat16),
-            pltpu.VMEM((here, length), jnp.bfloat16),
-            pltpu.VMEM((here, extent), f32),
-            pltpu.VMEM((rows, 2, length + 128), f32),
-            pltpu.VMEM((cols, 2, length + 128), f32),
-            pltpu.VMEM((rows, 2, length), f32),
-            dma((per_row,)),
-            dma((per_row,)),
-            dma((per_row,)),
-            dma((per_row,)),
-            dma((per_col,)),
-            dma((per_col,)),
-            dma((per_row,)),
-            dma((per_row,)),
-        ],
-        compiler_params=pltpu.CompilerParams(collective_id=0, has_side_effects=True),
-    )(residual, direction, coarse, fine, eigen, ground_shift.reshape(1, 1), previous.reshape(1, 1))
-    return output, ratio.reshape(1)
+        in_specs=[hbm] * 6,
+        out_specs=(vmem, vmem),
+        scratch_shapes=scratch,
+        compiler_params=pltpu.CompilerParams(
+            collective_id=0, has_side_effects=True, vmem_limit_bytes=min(held + (held >> 2) + (4 << 20), 60 << 20)
+        ),
+    )(residual, coarse, fine, eigen, ground_shift, previous)
+    return pl.pallas_call(
+        update,
+        out_shape=(
+            jax.ShapeDtypeStruct((extent, here), f32),
+            jax.ShapeDtypeStruct((1,), f32),
+        ),
+        in_specs=[vmem, vmem, vmem],
+        out_specs=(vmem, smem),
+        compiler_params=pltpu.CompilerParams(vmem_limit_bytes=8 * 1024 * 1024),
+    )(solved, direction, ratio)
+
+
+def update(solved_ref, direction_ref, ratio_in, out_ref, ratio_out):
+    ratio = ratio_in[0:1, 0:1]
+    out_ref[...] = solved_ref[...] + ratio * direction_ref[...]
+    ratio_out[0] = ratio_in[0, 0]
 
 
 def solution(mesh):

time: 32.1 us -> 31.4 us (0.978)
  local copies, waits for them, and re-layouts: 1.87 us -> 3.73 us
  between operations: 3.63 us -> 1.95 us
  Pallas kernels: 26.4 us -> 25.4 us
    pallas_call x1, Pallas kernels: 26.4 us -> 24.4 us  [body(): pl.pallas_call(functools.partial(kernel, rows, cols), out_shape=(jax.Shap...]
    unnamed x1 -> x10, local copies, waits for them, and re-layouts: 1.87 us -> 3.73 us
    pallas_call x0 -> x1, Pallas kernels: none -> 0.96 us  [body(): pl.pallas_call(update, out_shape=(jax.ShapeDtypeStruct((extent, here), f3...]
where the time goes in v1:
time: 31.4 us; the launch traced here: 31.1 us
  Pallas kernels  25.4 us (81%)
  local copies, waits for them, and re-layouts  3.73 us (12%)
  between operations  1.95 us (6%)
    pallas_call x1, Pallas kernels, body(): pl.pallas_call(functools.partial(kernel, rows, cols), out_shape=(jax.Shap...  24.4 us
    unnamed x10, local copies, waits for them, and re-layouts  3.73 us
    pallas_call x1, Pallas kernels, body(): pl.pallas_call(update, out_shape=(jax.ShapeDtypeStruct((extent, here), f3...  0.96 us

profile of v1, /device:TPU:0, one launch (start us, length us, event | category | flops | bytes accessed | tf_op | source)
XLA Modules:
  0.0 31.1 jit_solution(3562156597126014192)
XLA Ops:
  1.9 0.0 copy-start
  1.9 1.0 %copy-done = f32[256,512]{1,0:T(8,128)S(1)} copy-done((f32[256,512]{1,0:T(8,128)S(1)}, f32[256,512]{1,0:T(8,128)}, u32[]{:S(2)}) %copy-start) | copy-done | bytes 524312
  3.0 0.0 copy-start.1
  3.0 1.0 %copy-done.1 = f32[4,256,128]{2,1,0:T(8,128)S(1)} copy-done((f32[4,256,128]{2,1,0:T(8,128)S(1)}, f32[4,256,128]{2,1,0:T(8,128)}, u32[]{:S(2)}) %copy-start.1) | copy-done | bytes 524312
  4.0 0.0 copy-start.3
  4.0 0.9 %copy-done.3 = f32[2,256,128]{2,1,0:T(8,128)S(1)} copy-done((f32[2,256,128]{2,1,0:T(8,128)S(1)}, f32[2,256,128]{2,1,0:T(8,128)}, u32[]{:S(2)}) %copy-start.3) | copy-done | bytes 262168
  5.0 0.0 copy-start.4
  5.0 0.7 %copy-done.4 = f32[1,2048]{1,0:T(1,128)S(1)} copy-done((f32[1,2048]{1,0:T(1,128)S(1)}, f32[1,2048]{1,0:T(1,128)}, u32[]{:S(2)}) %copy-start.4) | copy-done | bytes 8216
  5.7 0.0 copy-start.2
  5.7 24.4 %shard_map.86 = (f32[256,512]{1,0:T(8,128)S(1)}, f32[1,128]{1,0:T(1,128)S(1)}) custom-call(f32[256,512]{1,0:T(8,128)S(1)} %copy-done, f32[4,256,128]{2,1,0:T(8,128)S(1)} %copy-done.1, f32[2,256,128]{2,1,0:T(8,128)S(1)} %copy-done.3, f32[1,2048]{1,0:T(1,128)S(1)} %copy-done.4, f32[1]{0:T(128)S(6)} %copy.9.shift_hbm, f32[1]{0:T(128)S(6)} %copy.10.previous_hbm), custom_call_target="tpu_custom_call" | custom-call | tf_op jit(solution)/shard_map/pallas_call | solution.py:435
  30.1 0.0 copy-done.2
  30.1 1.0 %shard_map.87 = (f32[256,512]{1,0:T(8,128)}, f32[1]{0:T(128)}) custom-call(f32[256,512]{1,0:T(8,128)S(1)} %get-tuple-element.4.solved_ref, f32[256,512]{1,0:T(8,128)S(1)} %copy-done.2, f32[1,128]{1,0:T(1,128)S(1)} %get-tuple-element.5.ratio_in), custom_call_target="tpu_custom_call" | custom-call | tf_op jit(solution)/shard_map/pallas_call | solution.py:448
Async XLA Ops:
  1.9 1.0 %copy-start = (f32[256,512]{1,0:T(8,128)S(1)}, f32[256,512]{1,0:T(8,128)}, u32[]{:S(2)}) copy-start(f32[256,512]{1,0:T(8,128)} %residual_hbm.1) | copy-start | bytes 1572868
  3.0 1.0 %copy-start.1 = (f32[4,256,128]{2,1,0:T(8,128)S(1)}, f32[4,256,128]{2,1,0:T(8,128)}, u32[]{:S(2)}) copy-start(f32[4,256,128]{2,1,0:T(8,128)} %constant.6.clone.coarse_hbm) | copy-start | bytes 1572868
  4.0 0.9 %copy-start.3 = (f32[2,256,128]{2,1,0:T(8,128)S(1)}, f32[2,256,128]{2,1,0:T(8,128)}, u32[]{:S(2)}) copy-start(f32[2,256,128]{2,1,0:T(8,128)} %constant.7.clone.fine_hbm) | copy-start | bytes 786436
  5.0 0.7 %copy-start.4 = (f32[1,2048]{1,0:T(1,128)S(1)}, f32[1,2048]{1,0:T(1,128)}, u32[]{:S(2)}) copy-start(f32[1,2048]{1,0:T(1,128)} %constant.8.clone.eigen_hbm) | copy-start | bytes 24580
  5.7 24.4 %copy-start.2 = (f32[256,512]{1,0:T(8,128)S(1)}, f32[256,512]{1,0:T(8,128)}, u32[]{:S(2)}) copy-start(f32[256,512]{1,0:T(8,128)} %direction_ref.1) | copy-start | bytes 1572868

commit v2 on v1

--- a/solution.py
+++ b/solution.py
@@ -73,16 +73,13 @@
     coarse_hbm,
     fine_hbm,
     eigen_hbm,
-    shift_hbm,
-    previous_hbm,
+    scalars_ref,
     out_ref,
     ratio_ref,
     residual_ref,
     coarse_ref,
     fine_ref,
     eigen_ref,
-    shift_ref,
-    previous_ref,
     load_sems,
     out1,
     in1,
@@ -136,8 +133,6 @@
             (coarse_hbm, coarse_ref),
             (fine_hbm, fine_ref),
             (eigen_hbm, eigen_ref),
-            (shift_hbm, shift_ref),
-            (previous_hbm, previous_ref),
         )
     ):
         copy = pltpu.make_async_copy(source, landing, load_sems.at[i])
@@ -205,7 +200,7 @@
 
     for copy in loads[3:]:
         copy.wait()
-    alpha = eigen_ref[...] + shift_ref[0]
+    alpha = eigen_ref[...] + scalars_ref[0:1, 0:1]
     h = 0.5 * jnp.sqrt(alpha)
     z = h / (1.0 + jnp.sqrt(1.0 + h * h))
     z2 = z * z
@@ -345,7 +340,7 @@
         coupled = coupled + lefts[k] * colsum[k, 1:2, :length] + rights[k] * colsum[k, 0:1, :length]
         inner = inner + colsum[k, 0:1, spare]
     inner = jnp.sum(inner + fold(weight * coupled), axis=1, keepdims=True)
-    ratio = inner / previous_ref[0]
+    ratio = inner / scalars_ref[1:2, 0:1]
     ratio_ref[...] = jnp.broadcast_to(ratio, ratio_ref.shape)
     for k in range(rows):
         carry[k, 0:1, :] = carry[k, 0:1, :] + left_c
@@ -398,9 +393,7 @@
         pltpu.VMEM(coarse.shape, f32),
         pltpu.VMEM(fine.shape, f32),
         pltpu.VMEM(eigen.shape, f32),
-        pltpu.SMEM((1,), f32),
-        pltpu.SMEM((1,), f32),
-        dma((6,)),
+        dma((4,)),
         pltpu.VMEM((rows, width, extent), f32),
         pltpu.VMEM((rows, width, extent), f32),
         pltpu.VMEM((rows, width, extent), f32),
@@ -432,19 +425,23 @@
         for ref in scratch
         if ref.memory_space == pltpu.VMEM
     )
+    scalars = jnp.broadcast_to(jnp.stack([ground_shift, previous]), (2, 128))
+    operands = (residual, coarse, fine, eigen)
     solved, ratio = pl.pallas_call(
         functools.partial(kernel, rows, cols),
         out_shape=(
             jax.ShapeDtypeStruct((extent, here), f32),
             jax.ShapeDtypeStruct((1, 128), f32),
         ),
-        in_specs=[hbm] * 6,
+        in_specs=[hbm] * 4 + [vmem],
         out_specs=(vmem, vmem),
         scratch_shapes=scratch,
         compiler_params=pltpu.CompilerParams(
-            collective_id=0, has_side_effects=True, vmem_limit_bytes=min(held + (held >> 2) + (4 << 20), 60 << 20)
+            collective_id=0,
+            has_side_effects=True,
+            vmem_limit_bytes=min(held + (held >> 2) + (4 << 20), 60 << 20),
         ),
-    )(residual, coarse, fine, eigen, ground_shift, previous)
+    )(*(pltpu.with_memory_space_constraint(x, pltpu.HBM) for x in operands), scalars)
     return pl.pallas_call(
         update,
         out_shape=(

time: 31.4 us -> 27.5 us (0.88)
  local copies, waits for them, and re-layouts: 3.73 us -> 0.08 us
    unnamed x10 -> x2, local copies, waits for them, and re-layouts: 3.73 us -> 0.01 us
where the time goes in v2:
time: 27.5 us; the launch traced here: 27.3 us
  Pallas kernels  25.2 us (92%)
  between operations  1.94 us (7%)
    pallas_call x1, Pallas kernels, body(): pl.pallas_call(functools.partial(kernel, rows, cols), out_shape=(jax.Shap...  24.3 us
    pallas_call x1, Pallas kernels, body(): pl.pallas_call(update, out_shape=(jax.ShapeDtypeStruct((extent, here), f3...  0.95 us

profile of v2, /device:TPU:0, one launch (start us, length us, event | category | flops | bytes accessed | tf_op | source)
XLA Modules:
  0.0 27.3 jit_solution(13075628409713533272)
XLA Ops:
  1.9 0.1 maximum_bitcast_fusion
  2.0 0.1 broadcast_in_dim.8.scalars_ref
  2.1 0.0 copy-start
  2.1 24.3 %shard_map.86 = (f32[256,512]{1,0:T(8,128)S(1)}, f32[1,128]{1,0:T(1,128)S(1)}) custom-call(f32[256,512]{1,0:T(8,128)} %residual_hbm.1, f32[4,256,128]{2,1,0:T(8,128)} %constant.6.clone.coarse_hbm, f32[2,256,128]{2,1,0:T(8,128)} %constant.7.clone.fine_hbm, f32[1,2048]{1,0:T(1,128)} %constant.8.clone.eigen_hbm, f32[2,128]{1,0:T(2,128)S(1)} %broadcast_in_dim.8.scalars_ref), custom_call_target="tpu_custom_call" | custom-call | tf_op jit(solution)/shard_map/pallas_call | solution.py:430
  26.4 0.0 copy-done
  26.4 0.9 %shard_map.87 = (f32[256,512]{1,0:T(8,128)}, f32[1]{0:T(128)}) custom-call(f32[256,512]{1,0:T(8,128)S(1)} %get-tuple-element.4.solved_ref, f32[256,512]{1,0:T(8,128)S(1)} %copy-done, f32[1,128]{1,0:T(1,128)S(1)} %get-tuple-element.5.ratio_in), custom_call_target="tpu_custom_call" | custom-call | tf_op jit(solution)/shard_map/pallas_call | solution.py:445
Async XLA Ops:
  2.1 24.3 %copy-start = (f32[256,512]{1,0:T(8,128)S(1)}, f32[256,512]{1,0:T(8,128)}, u32[]{:S(2)}) copy-start(f32[256,512]{1,0:T(8,128)} %direction_ref.1) | copy-start | bytes 1572868

commit v3 on v2

v3 whole, which is shorter than its diff:
```python
import functools
import math

import jax
import jax.numpy as jnp
import numpy as np
from jax import lax
from jax.experimental import pallas as pl
from jax.experimental.pallas import tpu as pltpu
from jax.sharding import PartitionSpec as P

MESH = pl.DeviceIdType.MESH
HALVES = 2


def halves_of(table):
    high = table.astype(jnp.bfloat16)
    low = (table - high.astype(np.float64)).astype(jnp.bfloat16)
    return np.stack([high, low])


def sine_table(extent):
    index = np.arange(1, extent + 1, dtype=np.int64)
    turns = index[:, None] * index[None, :] % (2 * (extent + 1))
    table = math.sqrt(2.0 / (extent + 1)) * np.sin(np.pi * turns / (extent + 1))
    eigen = 4.0 * np.sin(np.pi * index / (2 * (extent + 1))) ** 2
    return halves_of(table), eigen


def tables(extent, width, cols):
    length = width * cols
    modes = np.arange(length, dtype=np.int64)[None, :]
    coarse = 64 * np.arange(length // 64, dtype=np.int64)[:, None]
    middle = 8 * np.arange(8, dtype=np.int64)[:, None]
    fine = 2 * np.arange(8, dtype=np.int64)[:, None] + 1
    coarse = np.pi * (modes * coarse % (2 * length)) / length
    middle = np.pi * (modes * middle % (2 * length)) / length
    fine = np.pi * (modes * fine % (4 * length)) / (2 * length)
    scale = np.where(modes == 0, math.sqrt(1.0 / length), math.sqrt(2.0 / length))
    far = np.stack([np.cos(coarse), np.sin(coarse)]).astype(np.float32)
    near = np.stack(
        [np.cos(middle), np.sin(middle), scale * np.cos(fine), scale * np.sin(fine)]
    ).astype(np.float32)
    waves = 4.0 * np.sin(np.pi * modes / (2 * length)) ** 2
    row_sines, row_eigen = sine_table(extent)
    col_sines, col_eigen = sine_table(width)
    both = (col_eigen[:, None] + row_eigen[None, :]).astype(np.float32)
    return (
        far,
        near,
        waves.reshape(-1, 128).astype(np.float32),
        row_eigen[None, :].astype(np.float32),
        both,
        row_sines,
        col_sines,
    )


def split(value):
    high = value.astype(jnp.bfloat16)
    return high, (value - high.astype(jnp.float32)).astype(jnp.bfloat16)


def decay(alpha):
    h = 0.5 * jnp.sqrt(alpha)
    z = h / (1.0 + jnp.sqrt(1.0 + h * h))
    z2 = z * z
    series = jnp.full_like(z, 1.0 / 23)
    for p in range(21, 0, -2):
        series = series * z2 + 1.0 / p
    return 4.0 * z * series, 0.5 / jnp.sqrt(alpha * (1.0 + 0.25 * alpha))


def waves(ps, qs, chunk, whole):
    count = len(ps)
    fronts, backs = [], [None] * count
    left, right = jnp.zeros_like(chunk), jnp.zeros_like(chunk)
    for k in range(count):
        fronts.append(left)
        left = chunk * left + qs[k]
        backs[count - 1 - k] = right
        right = chunk * right + ps[count - 1 - k]
    images = 1.0 / (1.0 - whole * whole)
    entry = (right + whole * left) * images
    exit_ = (left + whole * right) * images
    for k in range(count):
        fronts[k] = fronts[k] + entry
        backs[count - 1 - k] = backs[count - 1 - k] + exit_
        entry, exit_ = entry * chunk, exit_ * chunk
    return fronts, backs


def amplitudes(ps, qs, theta, gain, extent, me):
    count = len(ps)
    fronts, backs = waves(
        ps, qs, jnp.exp(-theta * float(extent)), jnp.exp(-theta * float(extent * count))
    )
    far = jnp.exp(-theta * float(extent + 1))
    inside = gain / (1.0 - far * far)
    outside = gain * jnp.exp(theta)
    total = jnp.zeros_like(theta)
    mine_a, mine_b = jnp.zeros_like(theta), jnp.zeros_like(theta)
    for k in range(count):
        a = outside * fronts[k] + inside * (ps[k] - far * qs[k])
        b = outside * backs[k] + inside * (qs[k] - far * ps[k])
        total = total + a * ps[k] + b * qs[k]
        mine_a = jnp.where(me == k, a, mine_a)
        mine_b = jnp.where(me == k, b, mine_b)
    return mine_a, mine_b, total


def fill_decays(theta_rows, down_ref, up_ref):
    blocks = down_ref.shape[0] // 8
    tiles = len(theta_rows)
    place = lax.broadcasted_iota(jnp.int32, (8, 128), 0).astype(jnp.float32)
    for first in range(0, tiles, 8):
        group = range(first, min(first + 8, tiles))
        steps = [jnp.exp(-8.0 * jnp.broadcast_to(theta_rows[t], (8, 128))) for t in group]
        down = [jnp.exp(-theta_rows[t] * (place + 1.0)) for t in group]
        up = [jnp.exp(-theta_rows[t] * (8.0 - place)) for t in group]

        def step(n, carry):
            down, up = carry
            top = pl.ds(pl.multiple_of(8 * n, 8), 8)
            bottom = pl.ds(pl.multiple_of(8 * (blocks - 1 - n), 8), 8)
            for i, t in enumerate(group):
                down_ref[top, t * 128 : (t + 1) * 128] = down[i]
                up_ref[bottom, t * 128 : (t + 1) * 128] = up[i]
            return (
                [d * s for d, s in zip(down, steps)],
                [u * s for u, s in zip(up, steps)],
            )

        lax.fori_loop(0, blocks, step, (down, up))


def kernel(
    rows,
    cols,
    residual_hbm,
    far_hbm,
    near_hbm,
    waves_hbm,
    row_eigen_hbm,
    both_hbm,
    row_sines_hbm,
    col_sines_hbm,
    scalars_ref,
    out_ref,
    ratio_ref,
    residual_ref,
    far_ref,
    near_ref,
    waves_ref,
    row_eigen_ref,
    both_ref,
    row_sines_ref,
    col_sines_ref,
    load_sems,
    theta_ref,
    cos_ref,
    sin_ref,
    table_hi,
    table_lo,
    down,
    up,
    side_down,
    side_up,
    amp_ref,
    col_in,
    carry_in,
    row_in,
    quad_in,
    s_col,
    r_col,
    s_carry,
    r_carry,
    s_row,
    r_row,
    s_quad,
    r_quad,
):
    me_r = lax.axis_index("row")
    me_c = lax.axis_index("col")
    extent, width = residual_ref.shape
    length = table_hi.shape[1]
    tiles = length // 128
    part = tiles // HALVES
    f32 = jnp.float32

    barrier = pltpu.get_barrier_semaphore()
    for o in range(1, cols):
        pl.semaphore_signal(
            barrier, inc=1, device_id={"col": lax.rem(me_c + o, cols)}, device_id_type=MESH
        )
    for o in range(1, rows):
        pl.semaphore_signal(
            barrier, inc=1, device_id={"row": lax.rem(me_r + o, rows)}, device_id_type=MESH
        )

    per = width // 64
    own = far_hbm.at[:, pl.ds(pl.multiple_of(me_c * per, per), per), :]
    loads = []
    for i, (source, landing) in enumerate(
        (
            (waves_hbm, waves_ref),
            (near_hbm, near_ref),
            (own, far_ref),
            (residual_hbm, residual_ref),
            (row_eigen_hbm, row_eigen_ref),
            (row_sines_hbm, row_sines_ref),
            (col_sines_hbm, col_sines_ref),
            (both_hbm, both_ref),
        )
    ):
        copy = pltpu.make_async_copy(source, landing, load_sems.at[i])
        copy.start()
        loads.append(copy)

    def share(axis, me, count, ref, send_sems, recv_sems, first=0):
        copies = []
        for o in range(1, count):
            copy = pltpu.make_async_remote_copy(
                src_ref=ref,
                dst_ref=ref,
                send_sem=send_sems.at[first + o - 1],
                recv_sem=recv_sems.at[first + o - 1],
                device_id={axis: lax.rem(me + o, count)},
                device_id_type=MESH,
            )
            copy.start()
            copies.append(copy)
        return copies

    shift = scalars_ref[0:1, 0:1]
    loads[0].wait()
    theta, gain = decay(waves_ref[...] + shift)
    theta_ref[...] = theta
    fill_decays([theta_ref[t : t + 1, :] for t in range(tiles)], down, up)

    loads[1].wait()
    loads[2].wait()
    for u in range(per):
        rows_u = slice(8 * u, 8 * u + 8)
        cos_u, sin_u = far_ref[0, u : u + 1, :], far_ref[1, u : u + 1, :]
        cos_ref[rows_u, :] = cos_u * near_ref[0] - sin_u * near_ref[1]
        sin_ref[rows_u, :] = sin_u * near_ref[0] + cos_u * near_ref[1]

    span = min(1024, length)

    def fill(n, carry):
        at = pl.ds(pl.multiple_of(16 * n, 16), 16)
        for first in range(0, length, span):
            lanes = slice(first, first + span)
            pieces = []
            for k in range(2):
                row = pl.ds(2 * n + k, 1)
                pieces.append(
                    cos_ref[row, lanes] * near_ref[2, :, lanes]
                    - sin_ref[row, lanes] * near_ref[3, :, lanes]
                )
            high, low = split(jnp.concatenate(pieces, axis=0))
            table_hi[at, lanes] = high
            table_lo[at, lanes] = low
        return carry

    lax.fori_loop(0, width // 16, fill, 0)

    loads[3].wait()
    r_hi, r_lo = split(residual_ref[...])
    stacked = jnp.concatenate([r_hi, r_lo, r_hi], axis=1)
    for first in range(0, length, 256):
        lanes = slice(first, first + 256)
        high, low = table_hi[:, lanes], table_lo[:, lanes]
        value = jnp.dot(
            stacked, jnp.concatenate([high, high, low], axis=0), preferred_element_type=f32
        )
        p = jnp.sum(value * down[:, lanes], axis=0, keepdims=True)
        q = jnp.sum(value * up[:, lanes], axis=0, keepdims=True)
        for i in range(2):
            half, at = divmod(first // 128 + i, part)
            piece = slice(128 * i, 128 * i + 128)
            col_in[me_c, half, at : at + 1, :] = p[:, piece]
            col_in[me_c, half, part + at : part + at + 1, :] = q[:, piece]

    pl.semaphore_wait(barrier, rows + cols - 2)
    col_copies = [
        share("col", me_c, cols, col_in.at[me_c, h], s_col, r_col, h * (cols - 1))
        for h in range(HALVES)
    ]

    for copy in loads[4:]:
        copy.wait()
    left = (((0,), (0,)), ((), ()))
    turn = (((1,), (1,)), ((), ()))
    modal = lax.dot_general(
        jnp.concatenate([r_hi, r_lo, r_hi], axis=0),
        jnp.concatenate([row_sines_ref[0], row_sines_ref[0], row_sines_ref[1]], axis=0),
        left,
        preferred_element_type=f32,
    )
    phi, side_gain = decay(row_eigen_ref[...] + shift)
    fill_decays(
        [phi[:, e : e + 128] for e in range(0, extent, 128)], side_down, side_up
    )
    carry_in[me_c, 0:1, :] = jnp.sum(modal * side_down[...], axis=0, keepdims=True)
    carry_in[me_c, 1:2, :] = jnp.sum(modal * side_up[...], axis=0, keepdims=True)
    sines = jnp.concatenate([col_sines_ref[0], col_sines_ref[0], col_sines_ref[1]], axis=1)

    def across(value):
        high, low = split(value)
        return jnp.dot(
            sines, jnp.concatenate([high, low, high], axis=0), preferred_element_type=f32
        )

    spectrum = across(modal)
    scaled = spectrum / (both_ref[...] + shift)
    carry_in[me_c, 2:3, :] = jnp.sum(spectrum * scaled, axis=0, keepdims=True)
    carry_in[me_c, 3:4, :] = jnp.zeros((1, extent), f32)
    carry_copies = share("col", me_c, cols, carry_in.at[me_c], s_carry, r_carry)
    field = across(scaled)

    row_copies = []
    for h in range(HALVES):
        for copy in col_copies[h]:
            copy.wait_recv()
        total = col_in[0, h]
        for k in range(1, cols):
            total = total + col_in[k, h]
        row_in[me_r, h] = total
        row_copies.append(
            share("row", me_r, rows, row_in.at[me_r, h], s_row, r_row, h * (rows - 1))
        )

    for copy in carry_copies:
        copy.wait_recv()
    a, b, quad = amplitudes(
        [carry_in[k, 0:1, :] for k in range(cols)],
        [carry_in[k, 1:2, :] for k in range(cols)],
        phi,
        side_gain,
        width,
        me_c,
    )
    for k in range(cols):
        quad = quad + carry_in[k, 2:3, :]
    quad_in[me_r] = sum(quad[:, e : e + 128] for e in range(0, extent, 128))
    quad_copies = share("row", me_r, rows, quad_in.at[me_r], s_quad, r_quad)
    high, low = split(field + a * side_down[...] + b * side_up[...])
    out_ref[...] = lax.dot_general(
        jnp.concatenate([row_sines_ref[0], row_sines_ref[0], row_sines_ref[1]], axis=1),
        jnp.concatenate([high, low, high], axis=1),
        turn,
        preferred_element_type=f32,
    )

    inner = jnp.zeros((part, 128), f32)
    for h in range(HALVES):
        for copy in row_copies[h]:
            copy.wait_recv()
        at = slice(h * part, (h + 1) * part)
        a, b, quad = amplitudes(
            [row_in[k, h, :part] for k in range(rows)],
            [row_in[k, h, part:] for k in range(rows)],
            theta[at],
            gain[at],
            extent,
            me_r,
        )
        inner = inner + quad
        amp_ref[0, at] = a
        amp_ref[1, at] = b
        for first in range(h * part * 128, (h + 1) * part * 128, 256):
            lanes = slice(first, first + 256)
            t = first // 128
            a_row = jnp.concatenate([amp_ref[0, t + i : t + i + 1, :] for i in range(2)], axis=1)
            b_row = jnp.concatenate([amp_ref[1, t + i : t + i + 1, :] for i in range(2)], axis=1)
            high, low = split(a_row * down[:, lanes] + b_row * up[:, lanes])
            t_hi, t_lo = table_hi[:, lanes], table_lo[:, lanes]
            out_ref[...] += lax.dot_general(
                jnp.concatenate([high, low, high], axis=1),
                jnp.concatenate([t_hi, t_hi, t_lo], axis=1),
                turn,
                preferred_element_type=f32,
            )

    for copy in quad_copies:
        copy.wait_recv()
    inner = jnp.sum(inner, axis=0, keepdims=True)
    for k in range(rows):
        inner = inner + quad_in[k]
    ratio = jnp.sum(inner, axis=1, keepdims=True) / scalars_ref[1:2, 0:1]
    ratio_ref[...] = jnp.broadcast_to(ratio, ratio_ref.shape)
    for copies in (*col_copies, carry_copies, *row_copies, quad_copies):
        for copy in copies:
            copy.wait_send()


def body(rows, cols, residual, direction, ground_shift, previous):
    extent, width = residual.shape
    length = width * cols
    f32, bf16 = jnp.float32, jnp.bfloat16
    constants = tables(extent, width, cols)
    vmem = pl.BlockSpec(memory_space=pltpu.VMEM)
    smem = pl.BlockSpec(memory_space=pltpu.SMEM)
    hbm = pl.BlockSpec(memory_space=pltpu.HBM)
    dma = pltpu.SemaphoreType.DMA
    per_row, per_col = max(rows - 1, 1), max(cols - 1, 1)
    operands = (residual, *constants)
    scalars = jnp.broadcast_to(jnp.stack([ground_shift, previous]), (2, 128))
    tiles = length // 128
    part = tiles // HALVES
    landings = [
        pltpu.VMEM((2, width // 64, length) if i == 1 else x.shape, x.dtype)
        for i, x in enumerate(operands)
    ]
    scratch = landings + [
        dma((len(operands),)),
        pltpu.VMEM((tiles, 128), f32),
        pltpu.VMEM((width // 8, length), f32),
        pltpu.VMEM((width // 8, length), f32),
        pltpu.VMEM((width, length), bf16),
        pltpu.VMEM((width, length), bf16),
        pltpu.VMEM((extent, length), f32),
        pltpu.VMEM((extent, length), f32),
        pltpu.VMEM((width, extent), f32),
        pltpu.VMEM((width, extent), f32),
        pltpu.VMEM((2, tiles, 128), f32),
        pltpu.VMEM((cols, HALVES, 2 * part, 128), f32),
        pltpu.VMEM((cols, 4, extent), f32),
        pltpu.VMEM((rows, HALVES, 2 * part, 128), f32),
        pltpu.VMEM((rows, 1, 128), f32),
        dma((HALVES * per_col,)),
        dma((HALVES * per_col,)),
        dma((per_col,)),
        dma((per_col,)),
        dma((HALVES * per_row,)),
        dma((HALVES * per_row,)),
        dma((per_row,)),
        dma((per_row,)),
    ]
    held = sum(
        math.prod(ref.shape) * jnp.dtype(ref.dtype).itemsize
        for ref in scratch
        if ref.memory_space == pltpu.VMEM
    )
    solved, ratio = pl.pallas_call(
        functools.partial(kernel, rows, cols),
        out_shape=(
            jax.ShapeDtypeStruct((extent, width), f32),
            jax.ShapeDtypeStruct((1, 128), f32),
        ),
        in_specs=[hbm] * len(operands) + [vmem],
        out_specs=(vmem, vmem),
        scratch_shapes=scratch,
        compiler_params=pltpu.CompilerParams(
            collective_id=0,
            has_side_effects=True,
            vmem_limit_bytes=min(held + (held >> 2) + (8 << 20), 61 << 20),
        ),
    )(*(pltpu.with_memory_space_constraint(x, pltpu.HBM) for x in operands), scalars)
    return pl.pallas_call(
        update,
        out_shape=(
            jax.ShapeDtypeStruct((extent, width), f32),
            jax.ShapeDtypeStruct((1,), f32),
        ),
        in_specs=[vmem, vmem, vmem],
        out_specs=(vmem, smem),
        compiler_params=pltpu.CompilerParams(vmem_limit_bytes=8 << 20),
    )(solved, direction, ratio)


def update(solved_ref, direction_ref, ratio_in, out_ref, ratio_out):
    ratio = ratio_in[0:1, 0:1]
    out_ref[...] = solved_ref[...] + ratio * direction_ref[...]
    ratio_out[0] = ratio_in[0, 0]


def solution(mesh):
    return jax.shard_map(
        functools.partial(body, mesh.shape["row"], mesh.shape["col"]),
        mesh=mesh,
        in_specs=(P("row", "col"), P("row", "col"), P(), P()),
        out_specs=(P("row", "col"), P()),
        check_vma=False,
    )
```

time: 27.5 us -> 23.9 us (0.87)
  Pallas kernels: 25.2 us -> 21.7 us
    pallas_call x1, Pallas kernels: 24.3 us -> 20.7 us  [body(): pl.pallas_call(functools.partial(kernel, rows, cols), out_shape=(jax.Shap...]
where the time goes in v3:
time: 23.9 us; the launch traced here: 23.7 us
  Pallas kernels  21.7 us (91%)
  between operations  1.94 us (8%)
    pallas_call x1, Pallas kernels, body(): pl.pallas_call(functools.partial(kernel, rows, cols), out_shape=(jax.Shap...  20.7 us
    pallas_call x1, Pallas kernels, body(): pl.pallas_call(update, out_shape=(jax.ShapeDtypeStruct((extent, width), f...  0.96 us

profile of v3, /device:TPU:0, one launch (start us, length us, event | category | flops | bytes accessed | tf_op | source)
XLA Modules:
  0.0 23.7 jit_solution(314675269292374196)
XLA Ops:
  1.9 0.1 maximum_bitcast_fusion
  2.0 0.1 broadcast_in_dim.8.scalars_ref
  2.1 0.0 copy-start
  2.1 20.7 %shard_map.122 = (f32[256,512]{1,0:T(8,128)S(1)}, f32[1,128]{1,0:T(1,128)S(1)}) custom-call(f32[256,512]{1,0:T(8,128)} %residual_hbm.1, f32[2,32,2048]{2,1,0:T(8,128)} %constant.14.clone.far_hbm, f32[4,8,2048]{2,1,0:T(8,128)} %constant.15.clone.near_hbm, f32[16,128]{1,0:T(8,128)} %constant.16.clone.waves_hbm, f32[1,256]{1,0:T(1,128)} %constant.17.clone.row_eigen_hbm, ...), custom_call_target="tpu_custom_call" | custom-call | tf_op jit(solution)/shard_map/pallas_call | solution.py:447
  22.8 0.0 copy-done
  22.8 1.0 %shard_map.123 = (f32[256,512]{1,0:T(8,128)}, f32[1]{0:T(128)}) custom-call(f32[256,512]{1,0:T(8,128)S(1)} %get-tuple-element.4.solved_ref, f32[256,512]{1,0:T(8,128)S(1)} %copy-done, f32[1,128]{1,0:T(1,128)S(1)} %get-tuple-element.5.ratio_in), custom_call_target="tpu_custom_call" | custom-call | tf_op jit(solution)/shard_map/pallas_call | solution.py:462
Async XLA Ops:
  2.1 20.7 %copy-start = (f32[256,512]{1,0:T(8,128)S(1)}, f32[256,512]{1,0:T(8,128)}, u32[]{:S(2)}) copy-start(f32[256,512]{1,0:T(8,128)} %direction_ref.1) | copy-start | bytes 1572868

commit v4 on v3

--- a/solution.py
+++ b/solution.py
@@ -27,7 +27,16 @@
     return halves_of(table), eigen
 
 
-def tables(extent, width, cols):
+def column_cosines(width, cols):
+    length = width * cols
+    modes = np.arange(length, dtype=np.int64)[None, :]
+    odd = 2 * np.arange(length, dtype=np.int64)[:, None] + 1
+    scale = np.where(modes == 0, math.sqrt(1.0 / length), math.sqrt(2.0 / length))
+    table = scale * np.cos(np.pi * (modes * odd % (4 * length)) / (2 * length))
+    return halves_of(table).reshape(2, cols, width, length).swapaxes(0, 1)
+
+
+def tables(extent, width, cols, ready):
     length = width * cols
     modes = np.arange(length, dtype=np.int64)[None, :]
     coarse = 64 * np.arange(length // 64, dtype=np.int64)[:, None]
@@ -45,14 +54,14 @@
     row_sines, row_eigen = sine_table(extent)
     col_sines, col_eigen = sine_table(width)
     both = (col_eigen[:, None] + row_eigen[None, :]).astype(np.float32)
+    sources = (column_cosines(width, cols),) if ready else (far, near)
     return (
-        far,
-        near,
         waves.reshape(-1, 128).astype(np.float32),
         row_eigen[None, :].astype(np.float32),
         both,
         row_sines,
         col_sines,
+        *sources,
     )
 
 
@@ -134,56 +143,58 @@
         lax.fori_loop(0, blocks, step, (down, up))
 
 
-def kernel(
-    rows,
-    cols,
-    residual_hbm,
-    far_hbm,
-    near_hbm,
-    waves_hbm,
-    row_eigen_hbm,
-    both_hbm,
-    row_sines_hbm,
-    col_sines_hbm,
-    scalars_ref,
-    out_ref,
-    ratio_ref,
-    residual_ref,
-    far_ref,
-    near_ref,
-    waves_ref,
-    row_eigen_ref,
-    both_ref,
-    row_sines_ref,
-    col_sines_ref,
-    load_sems,
-    theta_ref,
-    cos_ref,
-    sin_ref,
-    table_hi,
-    table_lo,
-    down,
-    up,
-    side_down,
-    side_up,
-    amp_ref,
-    col_in,
-    carry_in,
-    row_in,
-    quad_in,
-    s_col,
-    r_col,
-    s_carry,
-    r_carry,
-    s_row,
-    r_row,
-    s_quad,
-    r_quad,
-):
+def kernel(rows, cols, ready, *refs):
+    def run(*sums):
+        apply(rows, cols, ready, sums, *refs)
+
+    extent = refs[0].shape[0]
+    pl.run_scoped(run, *(pltpu.ACC(m)((extent, 256), jnp.float32) for m in (0, 0, 1, 1)))
+
+
+def multiply(total, unit, right, left, transpose=False):
+    high, low = left
+    pltpu.matmul_push_rhs(right[0], 0, unit, transpose=transpose)
+    pltpu.matmul_acc_lhs(total, high, load_staged_rhs=0)
+    pltpu.matmul_acc_lhs(total, low)
+    pltpu.matmul_push_rhs(right[1], 1, unit, transpose=transpose)
+    pltpu.matmul_acc_lhs(total, high, load_staged_rhs=1)
+
+
+def apply(rows, cols, ready, sums, *refs):
+    sources = 1 if ready else 2
+    residual_hbm, waves_hbm, row_eigen_hbm, both_hbm, row_sines_hbm, col_sines_hbm = refs[:6]
+    source_hbms = refs[6 : 6 + sources]
+    scalars_ref, out_ref, ratio_ref = refs[6 + sources : 9 + sources]
+    residual_ref, waves_ref, row_eigen_ref, both_ref, row_sines_ref, col_sines_ref = refs[
+        9 + sources : 15 + sources
+    ]
+    (
+        load_sems,
+        theta_ref,
+        table,
+        down,
+        up,
+        side_down,
+        side_up,
+        amp_ref,
+        col_in,
+        carry_in,
+        row_in,
+        quad_in,
+        s_col,
+        r_col,
+        s_carry,
+        r_carry,
+        s_row,
+        r_row,
+        s_quad,
+        r_quad,
+        *spare,
+    ) = refs[15 + sources :]
     me_r = lax.axis_index("row")
     me_c = lax.axis_index("col")
     extent, width = residual_ref.shape
-    length = table_hi.shape[1]
+    length = table.shape[2]
     tiles = length // 128
     part = tiles // HALVES
     f32 = jnp.float32
@@ -198,24 +209,37 @@
             barrier, inc=1, device_id={"row": lax.rem(me_r + o, rows)}, device_id_type=MESH
         )
 
-    per = width // 64
-    own = far_hbm.at[:, pl.ds(pl.multiple_of(me_c * per, per), per), :]
     loads = []
-    for i, (source, landing) in enumerate(
-        (
-            (waves_hbm, waves_ref),
-            (near_hbm, near_ref),
-            (own, far_ref),
-            (residual_hbm, residual_ref),
+
+    def load(source, landing):
+        copy = pltpu.make_async_copy(source, landing, load_sems.at[len(loads)])
+        copy.start()
+        loads.append(copy)
+        return copy
+
+    waves_load = load(waves_hbm, waves_ref)
+    residual_load = load(residual_hbm, residual_ref)
+    chunk = min(512, length)
+    table_loads = []
+    if ready:
+        for first in range(0, length, chunk):
+            lanes = slice(first, first + chunk)
+            table_loads.append(load(source_hbms[0].at[me_c, :, :, lanes], table.at[:, :, lanes]))
+    else:
+        far_ref, near_ref, cos_ref, sin_ref = spare
+        per = width // 64
+        own = source_hbms[0].at[:, pl.ds(pl.multiple_of(me_c * per, per), per), :]
+        far_load = load(own, far_ref)
+        near_load = load(source_hbms[1], near_ref)
+    late_loads = [
+        load(source, landing)
+        for source, landing in (
             (row_eigen_hbm, row_eigen_ref),
             (row_sines_hbm, row_sines_ref),
             (col_sines_hbm, col_sines_ref),
             (both_hbm, both_ref),
         )
-    ):
-        copy = pltpu.make_async_copy(source, landing, load_sems.at[i])
-        copy.start()
-        loads.append(copy)
+    ]
 
     def share(axis, me, count, ref, send_sems, recv_sems, first=0):
         copies = []
@@ -233,52 +257,62 @@
         return copies
 
     shift = scalars_ref[0:1, 0:1]
-    loads[0].wait()
+    waves_load.wait()
     theta, gain = decay(waves_ref[...] + shift)
     theta_ref[...] = theta
     fill_decays([theta_ref[t : t + 1, :] for t in range(tiles)], down, up)
 
-    loads[1].wait()
-    loads[2].wait()
-    for u in range(per):
-        rows_u = slice(8 * u, 8 * u + 8)
-        cos_u, sin_u = far_ref[0, u : u + 1, :], far_ref[1, u : u + 1, :]
-        cos_ref[rows_u, :] = cos_u * near_ref[0] - sin_u * near_ref[1]
-        sin_ref[rows_u, :] = sin_u * near_ref[0] + cos_u * near_ref[1]
-
-    span = min(1024, length)
-
-    def fill(n, carry):
-        at = pl.ds(pl.multiple_of(16 * n, 16), 16)
-        for first in range(0, length, span):
-            lanes = slice(first, first + span)
-            pieces = []
-            for k in range(2):
-                row = pl.ds(2 * n + k, 1)
-                pieces.append(
-                    cos_ref[row, lanes] * near_ref[2, :, lanes]
-                    - sin_ref[row, lanes] * near_ref[3, :, lanes]
-                )
-            high, low = split(jnp.concatenate(pieces, axis=0))
-            table_hi[at, lanes] = high
-            table_lo[at, lanes] = low
-        return carry
-
-    lax.fori_loop(0, width // 16, fill, 0)
-
-    loads[3].wait()
+    if not ready:
+        far_load.wait()
+        near_load.wait()
+        for u in range(per):
+            rows_u = slice(8 * u, 8 * u + 8)
+            cos_u, sin_u = far_ref[0, u : u + 1, :], far_ref[1, u : u + 1, :]
+            cos_ref[rows_u, :] = cos_u * near_ref[0] - sin_u * near_ref[1]
+            sin_ref[rows_u, :] = sin_u * near_ref[0] + cos_u * near_ref[1]
+
+        span = min(1024, length)
+
+        def fill(n, carry):
+            at = pl.ds(pl.multiple_of(16 * n, 16), 16)
+            for first in range(0, length, span):
+                lanes = slice(first, first + span)
+                pieces = []
+                for k in range(2):
+                    row = pl.ds(2 * n + k, 1)
+                    pieces.append(
+                        cos_ref[row, lanes] * near_ref[2, :, lanes]
+                        - sin_ref[row, lanes] * near_ref[3, :, lanes]
+                    )
+                high, low = split(jnp.concatenate(pieces, axis=0))
+                table[0, at, lanes] = high
+                table[1, at, lanes] = low
+            return carry
+
+        lax.fori_loop(0, width // 16, fill, 0)
+
+    residual_load.wait()
     r_hi, r_lo = split(residual_ref[...])
-    stacked = jnp.concatenate([r_hi, r_lo, r_hi], axis=1)
-    for first in range(0, length, 256):
-        lanes = slice(first, first + 256)
-        high, low = table_hi[:, lanes], table_lo[:, lanes]
-        value = jnp.dot(
-            stacked, jnp.concatenate([high, high, low], axis=0), preferred_element_type=f32
-        )
+    for tile in range(length // 256):
+        lanes = slice(256 * tile, 256 * tile + 256)
+        if ready and tile in (0, 4):
+            for copy in table_loads[: 2] if tile == 0 else table_loads[2:]:
+                copy.wait()
+        unit = tile % 2
+        total = sums[2 * unit + tile // 2 % 2]
+        for first in range(0, width, 256):
+            at = slice(first, first + 256)
+            multiply(
+                total,
+                unit,
+                (table[0, at, lanes], table[1, at, lanes]),
+                (r_hi[:, at], r_lo[:, at]),
+            )
+        value = pltpu.matmul_pop(total)
         p = jnp.sum(value * down[:, lanes], axis=0, keepdims=True)
         q = jnp.sum(value * up[:, lanes], axis=0, keepdims=True)
         for i in range(2):
-            half, at = divmod(first // 128 + i, part)
+            half, at = divmod(2 * tile + i, part)
             piece = slice(128 * i, 128 * i + 128)
             col_in[me_c, half, at : at + 1, :] = p[:, piece]
             col_in[me_c, half, part + at : part + at + 1, :] = q[:, piece]
@@ -289,29 +323,36 @@
         for h in range(HALVES)
     ]
 
-    for copy in loads[4:]:
+    for copy in late_loads:
         copy.wait()
-    left = (((0,), (0,)), ((), ()))
-    turn = (((1,), (1,)), ((), ()))
-    modal = lax.dot_general(
-        jnp.concatenate([r_hi, r_lo, r_hi], axis=0),
-        jnp.concatenate([row_sines_ref[0], row_sines_ref[0], row_sines_ref[1]], axis=0),
-        left,
-        preferred_element_type=f32,
-    )
+    turned_hi, turned_lo = split(residual_ref[...].T)
+    tops = [slice(256 * unit, 256 * unit + 256) for unit in range(2)]
+    for unit in range(2):
+        multiply(
+            sums[2 * unit],
+            unit,
+            (row_sines_ref[0], row_sines_ref[1]),
+            (turned_hi[tops[unit]], turned_lo[tops[unit]]),
+        )
+    modal = jnp.concatenate([pltpu.matmul_pop(sums[2 * unit]) for unit in range(2)], axis=0)
     phi, side_gain = decay(row_eigen_ref[...] + shift)
     fill_decays(
         [phi[:, e : e + 128] for e in range(0, extent, 128)], side_down, side_up
     )
     carry_in[me_c, 0:1, :] = jnp.sum(modal * side_down[...], axis=0, keepdims=True)
     carry_in[me_c, 1:2, :] = jnp.sum(modal * side_up[...], axis=0, keepdims=True)
-    sines = jnp.concatenate([col_sines_ref[0], col_sines_ref[0], col_sines_ref[1]], axis=1)
 
     def across(value):
         high, low = split(value)
-        return jnp.dot(
-            sines, jnp.concatenate([high, low, high], axis=0), preferred_element_type=f32
-        )
+        for unit in range(2):
+            for at in tops:
+                multiply(
+                    sums[2 * unit],
+                    unit,
+                    (high[at], low[at]),
+                    (col_sines_ref[0, tops[unit], at], col_sines_ref[1, tops[unit], at]),
+                )
+        return jnp.concatenate([pltpu.matmul_pop(sums[2 * unit]) for unit in range(2)], axis=0)
 
     spectrum = across(modal)
     scaled = spectrum / (both_ref[...] + shift)
@@ -347,12 +388,15 @@
     quad_in[me_r] = sum(quad[:, e : e + 128] for e in range(0, extent, 128))
     quad_copies = share("row", me_r, rows, quad_in.at[me_r], s_quad, r_quad)
     high, low = split(field + a * side_down[...] + b * side_up[...])
-    out_ref[...] = lax.dot_general(
-        jnp.concatenate([row_sines_ref[0], row_sines_ref[0], row_sines_ref[1]], axis=1),
-        jnp.concatenate([high, low, high], axis=1),
-        turn,
-        preferred_element_type=f32,
-    )
+    for unit in range(2):
+        at = slice(256 * unit, 256 * unit + 256)
+        multiply(
+            sums[2 * unit],
+            unit,
+            (high[at], low[at]),
+            (row_sines_ref[0], row_sines_ref[1]),
+            transpose=True,
+        )
 
     inner = jnp.zeros((part, 128), f32)
     for h in range(HALVES):
@@ -376,13 +420,17 @@
             a_row = jnp.concatenate([amp_ref[0, t + i : t + i + 1, :] for i in range(2)], axis=1)
             b_row = jnp.concatenate([amp_ref[1, t + i : t + i + 1, :] for i in range(2)], axis=1)
             high, low = split(a_row * down[:, lanes] + b_row * up[:, lanes])
-            t_hi, t_lo = table_hi[:, lanes], table_lo[:, lanes]
-            out_ref[...] += lax.dot_general(
-                jnp.concatenate([high, low, high], axis=1),
-                jnp.concatenate([t_hi, t_hi, t_lo], axis=1),
-                turn,
-                preferred_element_type=f32,
-            )
+            for unit in range(2):
+                at = slice(256 * unit, 256 * unit + 256)
+                multiply(
+                    sums[2 * unit],
+                    unit,
+                    (table[0, at, lanes], table[1, at, lanes]),
+                    (high, low),
+                    transpose=True,
+                )
+    for unit in range(2):
+        out_ref[:, 256 * unit : 256 * unit + 256] = pltpu.matmul_pop(sums[2 * unit])
 
     for copy in quad_copies:
         copy.wait_recv()
@@ -400,7 +448,8 @@
     extent, width = residual.shape
     length = width * cols
     f32, bf16 = jnp.float32, jnp.bfloat16
-    constants = tables(extent, width, cols)
+    ready = 4 * length * length <= 1 << 24
+    constants = tables(extent, width, cols, ready)
     vmem = pl.BlockSpec(memory_space=pltpu.VMEM)
     smem = pl.BlockSpec(memory_space=pltpu.SMEM)
     hbm = pl.BlockSpec(memory_space=pltpu.HBM)
@@ -410,17 +459,10 @@
     scalars = jnp.broadcast_to(jnp.stack([ground_shift, previous]), (2, 128))
     tiles = length // 128
     part = tiles // HALVES
-    landings = [
-        pltpu.VMEM((2, width // 64, length) if i == 1 else x.shape, x.dtype)
-        for i, x in enumerate(operands)
-    ]
-    scratch = landings + [
-        dma((len(operands),)),
+    scratch = [pltpu.VMEM(x.shape, x.dtype) for x in operands[:6]] + [
+        dma((len(operands) + length // min(512, length),)),
         pltpu.VMEM((tiles, 128), f32),
-        pltpu.VMEM((width // 8, length), f32),
-        pltpu.VMEM((width // 8, length), f32),
-        pltpu.VMEM((width, length), bf16),
-        pltpu.VMEM((width, length), bf16),
+        pltpu.VMEM((2, width, length), bf16),
         pltpu.VMEM((extent, length), f32),
         pltpu.VMEM((extent, length), f32),
         pltpu.VMEM((width, extent), f32),
@@ -439,13 +481,20 @@
         dma((per_row,)),
         dma((per_row,)),
     ]
+    if not ready:
+        scratch += [
+            pltpu.VMEM((2, width // 64, length), f32),
+            pltpu.VMEM((4, 8, length), f32),
+            pltpu.VMEM((width // 8, length), f32),
+            pltpu.VMEM((width // 8, length), f32),
+        ]
     held = sum(
         math.prod(ref.shape) * jnp.dtype(ref.dtype).itemsize
         for ref in scratch
         if ref.memory_space == pltpu.VMEM
     )
     solved, ratio = pl.pallas_call(
-        functools.partial(kernel, rows, cols),
+        functools.partial(kernel, rows, cols, ready),
         out_shape=(
             jax.ShapeDtypeStruct((extent, width), f32),
             jax.ShapeDtypeStruct((1, 128), f32),

time: 23.9 us -> 20.7 us (0.87)
  Pallas kernels: 21.7 us -> 18.3 us
    pallas_call x1, Pallas kernels: 20.7 us -> 17.4 us  [body(): pl.pallas_call(functools.partial(kernel, rows, cols, ready), out_shape=(j...]
where the time goes in v4:
time: 20.7 us; the launch traced here: 20.5 us
  Pallas kernels  18.3 us (88%)
  between operations  2 us (10%)
    pallas_call x1, Pallas kernels, body(): pl.pallas_call(functools.partial(kernel, rows, cols, ready), out_shape=(j...  17.4 us
    pallas_call x1, Pallas kernels, body(): pl.pallas_call(update, out_shape=(jax.ShapeDtypeStruct((extent, width), f...  0.96 us

profile of v4, /device:TPU:0, one launch (start us, length us, event | category | flops | bytes accessed | tf_op | source)
XLA Modules:
  0.0 20.5 jit_solution(310270401768280525)
XLA Ops:
  0.6 0.0 copy-start
  2.0 0.1 maximum_bitcast_fusion
  2.1 0.1 broadcast_in_dim.8.refs_7_
  2.1 17.4 %shard_map.113 = (f32[256,512]{1,0:T(8,128)S(1)}, f32[1,128]{1,0:T(1,128)S(1)}) custom-call(f32[256,512]{1,0:T(8,128)} %refs_0_.1, f32[16,128]{1,0:T(8,128)} %constant.12.clone.refs_1_, f32[1,256]{1,0:T(1,128)} %constant.13.clone.refs_2_, f32[512,256]{1,0:T(8,128)} %constant.14.clone.refs_3_, bf16[2,256,256]{2,1,0:T(8,128)(2,1)} %constant.15.clone.refs_4_, ...), custom_call_target="tpu_custom_call" | custom-call | tf_op jit(solution)/shard_map/pallas_call | solution.py:496
  19.5 0.0 copy-done
  19.5 1.0 %shard_map.114 = (f32[256,512]{1,0:T(8,128)}, f32[1]{0:T(128)}) custom-call(f32[256,512]{1,0:T(8,128)S(1)} %get-tuple-element.4.solved_ref, f32[256,512]{1,0:T(8,128)S(1)} %copy-done, f32[1,128]{1,0:T(1,128)S(1)} %get-tuple-element.5.ratio_in), custom_call_target="tpu_custom_call" | custom-call | tf_op jit(solution)/shard_map/pallas_call | solution.py:511
Async XLA Ops:
  0.6 18.9 %copy-start = (f32[256,512]{1,0:T(8,128)S(1)}, f32[256,512]{1,0:T(8,128)}, u32[]{:S(2)}) copy-start(f32[256,512]{1,0:T(8,128)} %direction_ref.1) | copy-start | bytes 1572868

commit v5 on v4

--- a/solution.py
+++ b/solution.py
@@ -10,7 +10,7 @@
 from jax.sharding import PartitionSpec as P
 
 MESH = pl.DeviceIdType.MESH
-HALVES = 2
+PARTS = 2
 
 
 def halves_of(table):
@@ -118,15 +118,44 @@
     return mine_a, mine_b, total
 
 
-def fill_decays(theta_rows, down_ref, up_ref):
+def fill_decays(theta, lanes, down_ref, up_ref):
     blocks = down_ref.shape[0] // 8
-    tiles = len(theta_rows)
+    wide = (8, theta.shape[1])
+    place = lax.broadcasted_iota(jnp.int32, wide, 0).astype(jnp.float32)
+    step = jnp.exp(jnp.broadcast_to(-8.0 * theta, wide))
+    down = jnp.exp(-theta * (place + 1.0))
+    up = jnp.exp(-theta * (8.0 - place))
+    for n in range(blocks):
+        down_ref[8 * n : 8 * n + 8, lanes] = down
+        up_ref[8 * (blocks - 1 - n) : 8 * (blocks - n), lanes] = up
+        down, up = down * step, up * step
+
+
+def edge_sums(value, theta):
+    wide = (8, theta.shape[1])
+    place = lax.broadcasted_iota(jnp.int32, wide, 0).astype(jnp.float32)
+    step = jnp.exp(jnp.broadcast_to(-8.0 * theta, wide))
+    blocks = [value[i : i + 8] for i in range(0, value.shape[0], 8)]
+    up, down = blocks[0], blocks[-1]
+    for n in range(1, len(blocks)):
+        up = up * step + blocks[n]
+        down = down * step + blocks[-1 - n]
+    return (
+        jnp.sum(down * jnp.exp(-theta * (place + 1.0)), axis=0, keepdims=True),
+        jnp.sum(up * jnp.exp(-theta * (8.0 - place)), axis=0, keepdims=True),
+    )
+
+
+def fill_all(theta_ref, down_ref, up_ref):
+    blocks = down_ref.shape[0] // 8
+    tiles = theta_ref.shape[0]
     place = lax.broadcasted_iota(jnp.int32, (8, 128), 0).astype(jnp.float32)
     for first in range(0, tiles, 8):
         group = range(first, min(first + 8, tiles))
-        steps = [jnp.exp(-8.0 * jnp.broadcast_to(theta_rows[t], (8, 128))) for t in group]
-        down = [jnp.exp(-theta_rows[t] * (place + 1.0)) for t in group]
-        up = [jnp.exp(-theta_rows[t] * (8.0 - place)) for t in group]
+        thetas = [theta_ref[t : t + 1, :] for t in group]
+        steps = [jnp.exp(jnp.broadcast_to(-8.0 * theta, (8, 128))) for theta in thetas]
+        down = [jnp.exp(-theta * (place + 1.0)) for theta in thetas]
+        up = [jnp.exp(-theta * (8.0 - place)) for theta in thetas]
 
         def step(n, carry):
             down, up = carry
@@ -181,6 +210,7 @@
         carry_in,
         row_in,
         quad_in,
+        block_in,
         s_col,
         r_col,
         s_carry,
@@ -189,6 +219,8 @@
         r_row,
         s_quad,
         r_quad,
+        s_block,
+        r_block,
         *spare,
     ) = refs[15 + sources :]
     me_r = lax.axis_index("row")
@@ -196,7 +228,7 @@
     extent, width = residual_ref.shape
     length = table.shape[2]
     tiles = length // 128
-    part = tiles // HALVES
+    part = tiles // PARTS
     f32 = jnp.float32
 
     barrier = pltpu.get_barrier_semaphore()
@@ -260,7 +292,6 @@
     waves_load.wait()
     theta, gain = decay(waves_ref[...] + shift)
     theta_ref[...] = theta
-    fill_decays([theta_ref[t : t + 1, :] for t in range(tiles)], down, up)
 
     if not ready:
         far_load.wait()
@@ -291,37 +322,41 @@
 
         lax.fori_loop(0, width // 16, fill, 0)
 
-    residual_load.wait()
-    r_hi, r_lo = split(residual_ref[...])
-    for tile in range(length // 256):
-        lanes = slice(256 * tile, 256 * tile + 256)
-        if ready and tile in (0, 4):
-            for copy in table_loads[: 2] if tile == 0 else table_loads[2:]:
-                copy.wait()
-        unit = tile % 2
-        total = sums[2 * unit + tile // 2 % 2]
-        for first in range(0, width, 256):
-            at = slice(first, first + 256)
-            multiply(
-                total,
-                unit,
-                (table[0, at, lanes], table[1, at, lanes]),
-                (r_hi[:, at], r_lo[:, at]),
+    col_copies = []
+    for h in range(PARTS):
+        if ready:
+            for first in range(0, length, chunk):
+                if h == first * PARTS // length:
+                    table_loads[first // chunk].wait()
+        if h == 0:
+            residual_load.wait()
+            r_hi, r_lo = split(residual_ref[...])
+        for tile in range(h * part // 2, (h + 1) * part // 2):
+            lanes = slice(256 * tile, 256 * tile + 256)
+            unit = tile % 2
+            total = sums[2 * unit + tile // 2 % 2]
+            for first in range(0, width, 256):
+                at = slice(first, first + 256)
+                multiply(
+                    total,
+                    unit,
+                    (table[0, at, lanes], table[1, at, lanes]),
+                    (r_hi[:, at], r_lo[:, at]),
+                )
+            value = pltpu.matmul_pop(total)
+            p, q = edge_sums(
+                value, jnp.concatenate([theta_ref[2 * tile + i : 2 * tile + i + 1] for i in (0, 1)], axis=1)
             )
-        value = pltpu.matmul_pop(total)
-        p = jnp.sum(value * down[:, lanes], axis=0, keepdims=True)
-        q = jnp.sum(value * up[:, lanes], axis=0, keepdims=True)
-        for i in range(2):
-            half, at = divmod(2 * tile + i, part)
-            piece = slice(128 * i, 128 * i + 128)
-            col_in[me_c, half, at : at + 1, :] = p[:, piece]
-            col_in[me_c, half, part + at : part + at + 1, :] = q[:, piece]
-
-    pl.semaphore_wait(barrier, rows + cols - 2)
-    col_copies = [
-        share("col", me_c, cols, col_in.at[me_c, h], s_col, r_col, h * (cols - 1))
-        for h in range(HALVES)
-    ]
+            for i in range(2):
+                at = 2 * tile + i - h * part
+                piece = slice(128 * i, 128 * i + 128)
+                col_in[me_c, h, at : at + 1, :] = p[:, piece]
+                col_in[me_c, h, part + at : part + at + 1, :] = q[:, piece]
+        if h == 0:
+            pl.semaphore_wait(barrier, rows + cols - 2)
+        col_copies.append(
+            share("col", me_c, cols, col_in.at[me_c, h], s_col, r_col, h * (cols - 1))
+        )
 
     for copy in late_loads:
         copy.wait()
@@ -336,11 +371,10 @@
         )
     modal = jnp.concatenate([pltpu.matmul_pop(sums[2 * unit]) for unit in range(2)], axis=0)
     phi, side_gain = decay(row_eigen_ref[...] + shift)
-    fill_decays(
-        [phi[:, e : e + 128] for e in range(0, extent, 128)], side_down, side_up
-    )
+    fill_decays(phi, slice(0, extent), side_down, side_up)
     carry_in[me_c, 0:1, :] = jnp.sum(modal * side_down[...], axis=0, keepdims=True)
     carry_in[me_c, 1:2, :] = jnp.sum(modal * side_up[...], axis=0, keepdims=True)
+    carry_copies = share("col", me_c, cols, carry_in.at[me_c], s_carry, r_carry)
 
     def across(value):
         high, low = split(value)
@@ -356,13 +390,14 @@
 
     spectrum = across(modal)
     scaled = spectrum / (both_ref[...] + shift)
-    carry_in[me_c, 2:3, :] = jnp.sum(spectrum * scaled, axis=0, keepdims=True)
-    carry_in[me_c, 3:4, :] = jnp.zeros((1, extent), f32)
-    carry_copies = share("col", me_c, cols, carry_in.at[me_c], s_carry, r_carry)
+    block = jnp.sum(spectrum * scaled, axis=0, keepdims=True)
+    block_in[me_c] = sum(block[:, e : e + 128] for e in range(0, extent, 128))
+    block_copies = share("col", me_c, cols, block_in.at[me_c], s_block, r_block)
     field = across(scaled)
+    fill_all(theta_ref, down, up)
 
     row_copies = []
-    for h in range(HALVES):
+    for h in range(PARTS):
         for copy in col_copies[h]:
             copy.wait_recv()
         total = col_in[0, h]
@@ -383,10 +418,7 @@
         width,
         me_c,
     )
-    for k in range(cols):
-        quad = quad + carry_in[k, 2:3, :]
-    quad_in[me_r] = sum(quad[:, e : e + 128] for e in range(0, extent, 128))
-    quad_copies = share("row", me_r, rows, quad_in.at[me_r], s_quad, r_quad)
+    quad = sum(quad[:, e : e + 128] for e in range(0, extent, 128))
     high, low = split(field + a * side_down[...] + b * side_up[...])
     for unit in range(2):
         at = slice(256 * unit, 256 * unit + 256)
@@ -397,9 +429,15 @@
             (row_sines_ref[0], row_sines_ref[1]),
             transpose=True,
         )
+    for copy in block_copies:
+        copy.wait_recv()
+    for k in range(cols):
+        quad = quad + block_in[k]
+    quad_in[me_r] = quad
+    quad_copies = share("row", me_r, rows, quad_in.at[me_r], s_quad, r_quad)
 
     inner = jnp.zeros((part, 128), f32)
-    for h in range(HALVES):
+    for h in range(PARTS):
         for copy in row_copies[h]:
             copy.wait_recv()
         at = slice(h * part, (h + 1) * part)
@@ -416,6 +454,14 @@
         amp_ref[1, at] = b
         for first in range(h * part * 128, (h + 1) * part * 128, 256):
             lanes = slice(first, first + 256)
+            if first == length - 256:
+                for copy in quad_copies:
+                    copy.wait_recv()
+                inner = jnp.sum(inner, axis=0, keepdims=True)
+                for k in range(rows):
+                    inner = inner + quad_in[k]
+                ratio = jnp.sum(inner, axis=1, keepdims=True) / scalars_ref[1:2, 0:1]
+                ratio_ref[...] = jnp.broadcast_to(ratio, ratio_ref.shape)
             t = first // 128
             a_row = jnp.concatenate([amp_ref[0, t + i : t + i + 1, :] for i in range(2)], axis=1)
             b_row = jnp.concatenate([amp_ref[1, t + i : t + i + 1, :] for i in range(2)], axis=1)
@@ -431,15 +477,7 @@
                 )
     for unit in range(2):
         out_ref[:, 256 * unit : 256 * unit + 256] = pltpu.matmul_pop(sums[2 * unit])
-
-    for copy in quad_copies:
-        copy.wait_recv()
-    inner = jnp.sum(inner, axis=0, keepdims=True)
-    for k in range(rows):
-        inner = inner + quad_in[k]
-    ratio = jnp.sum(inner, axis=1, keepdims=True) / scalars_ref[1:2, 0:1]
-    ratio_ref[...] = jnp.broadcast_to(ratio, ratio_ref.shape)
-    for copies in (*col_copies, carry_copies, *row_copies, quad_copies):
+    for copies in (*col_copies, carry_copies, block_copies, *row_copies, quad_copies):
         for copy in copies:
             copy.wait_send()
 
@@ -458,7 +496,7 @@
     operands = (residual, *constants)
     scalars = jnp.broadcast_to(jnp.stack([ground_shift, previous]), (2, 128))
     tiles = length // 128
-    part = tiles // HALVES
+    part = tiles // PARTS
     scratch = [pltpu.VMEM(x.shape, x.dtype) for x in operands[:6]] + [
         dma((len(operands) + length // min(512, length),)),
         pltpu.VMEM((tiles, 128), f32),
@@ -468,18 +506,21 @@
         pltpu.VMEM((width, extent), f32),
         pltpu.VMEM((width, extent), f32),
         pltpu.VMEM((2, tiles, 128), f32),
-        pltpu.VMEM((cols, HALVES, 2 * part, 128), f32),
-        pltpu.VMEM((cols, 4, extent), f32),
-        pltpu.VMEM((rows, HALVES, 2 * part, 128), f32),
+        pltpu.VMEM((cols, PARTS, 2 * part, 128), f32),
+        pltpu.VMEM((cols, 2, extent), f32),
+        pltpu.VMEM((rows, PARTS, 2 * part, 128), f32),
         pltpu.VMEM((rows, 1, 128), f32),
-        dma((HALVES * per_col,)),
-        dma((HALVES * per_col,)),
+        pltpu.VMEM((cols, 1, 128), f32),
+        dma((PARTS * per_col,)),
+        dma((PARTS * per_col,)),
         dma((per_col,)),
         dma((per_col,)),
-        dma((HALVES * per_row,)),
-        dma((HALVES * per_row,)),
+        dma((PARTS * per_row,)),
+        dma((PARTS * per_row,)),
         dma((per_row,)),
         dma((per_row,)),
+        dma((per_col,)),
+        dma((per_col,)),
     ]
     if not ready:
         scratch += [

time: 20.7 us -> 20.1 us (0.971)
  Pallas kernels: 18.3 us -> 17.8 us
    pallas_call x1, Pallas kernels: 17.4 us -> 16.8 us  [body(): pl.pallas_call(functools.partial(kernel, rows, cols, ready), out_shape=(j...]
where the time goes in v5:
time: 20.1 us; the launch traced here: 19.9 us
  Pallas kernels  17.8 us (89%)
  between operations  2 us (10%)
    pallas_call x1, Pallas kernels, body(): pl.pallas_call(functools.partial(kernel, rows, cols, ready), out_shape=(j...  16.8 us
    pallas_call x1, Pallas kernels, body(): pl.pallas_call(update, out_shape=(jax.ShapeDtypeStruct((extent, width), f...  0.95 us

profile of v5, /device:TPU:0, one launch (start us, length us, event | category | flops | bytes accessed | tf_op | source)
XLA Modules:
  0.0 19.9 jit_solution(9400423443828769499)
XLA Ops:
  0.6 0.0 copy-start
  2.0 0.1 maximum_bitcast_fusion
  2.1 0.1 broadcast_in_dim.8.refs_7_
  2.1 16.8 %shard_map.113 = (f32[256,512]{1,0:T(8,128)S(1)}, f32[1,128]{1,0:T(1,128)S(1)}) custom-call(f32[256,512]{1,0:T(8,128)} %refs_0_.1, f32[16,128]{1,0:T(8,128)} %constant.12.clone.refs_1_, f32[1,256]{1,0:T(1,128)} %constant.13.clone.refs_2_, f32[512,256]{1,0:T(8,128)} %constant.14.clone.refs_3_, bf16[2,256,256]{2,1,0:T(8,128)(2,1)} %constant.15.clone.refs_4_, ...), custom_call_target="tpu_custom_call" | custom-call | tf_op jit(solution)/shard_map/pallas_call | solution.py:537
  19.0 0.0 copy-done
  19.0 0.9 %shard_map.114 = (f32[256,512]{1,0:T(8,128)}, f32[1]{0:T(128)}) custom-call(f32[256,512]{1,0:T(8,128)S(1)} %get-tuple-element.4.solved_ref, f32[256,512]{1,0:T(8,128)S(1)} %copy-done, f32[1,128]{1,0:T(1,128)S(1)} %get-tuple-element.5.ratio_in), custom_call_target="tpu_custom_call" | custom-call | tf_op jit(solution)/shard_map/pallas_call | solution.py:552
Async XLA Ops:
  0.6 18.3 %copy-start = (f32[256,512]{1,0:T(8,128)S(1)}, f32[256,512]{1,0:T(8,128)}, u32[]{:S(2)}) copy-start(f32[256,512]{1,0:T(8,128)} %direction_ref.1) | copy-start | bytes 1572868

commit v6 on v5

--- a/solution.py
+++ b/solution.py
@@ -251,6 +251,7 @@
 
     waves_load = load(waves_hbm, waves_ref)
     residual_load = load(residual_hbm, residual_ref)
+    early_loads = [load(row_eigen_hbm, row_eigen_ref), load(row_sines_hbm, row_sines_ref)]
     chunk = min(512, length)
     table_loads = []
     if ready:
@@ -266,8 +267,6 @@
     late_loads = [
         load(source, landing)
         for source, landing in (
-            (row_eigen_hbm, row_eigen_ref),
-            (row_sines_hbm, row_sines_ref),
             (col_sines_hbm, col_sines_ref),
             (both_hbm, both_ref),
         )
@@ -322,15 +321,31 @@
 
         lax.fori_loop(0, width // 16, fill, 0)
 
+    residual_load.wait()
+    for copy in early_loads:
+        copy.wait()
+    r_hi, r_lo = split(residual_ref[...])
+    turned_hi, turned_lo = split(residual_ref[...].T)
+    tops = [slice(256 * unit, 256 * unit + 256) for unit in range(2)]
+    for unit in range(2):
+        multiply(
+            sums[2 * unit],
+            unit,
+            (row_sines_ref[0], row_sines_ref[1]),
+            (turned_hi[tops[unit]], turned_lo[tops[unit]]),
+        )
+    modal = jnp.concatenate([pltpu.matmul_pop(sums[2 * unit]) for unit in range(2)], axis=0)
+    phi, side_gain = decay(row_eigen_ref[...] + shift)
+    fill_decays(phi, slice(0, extent), side_down, side_up)
+    carry_in[me_c, 0:1, :] = jnp.sum(modal * side_down[...], axis=0, keepdims=True)
+    carry_in[me_c, 1:2, :] = jnp.sum(modal * side_up[...], axis=0, keepdims=True)
+
     col_copies = []
     for h in range(PARTS):
         if ready:
             for first in range(0, length, chunk):
                 if h == first * PARTS // length:
                     table_loads[first // chunk].wait()
-        if h == 0:
-            residual_load.wait()
-            r_hi, r_lo = split(residual_ref[...])
         for tile in range(h * part // 2, (h + 1) * part // 2):
             lanes = slice(256 * tile, 256 * tile + 256)
             unit = tile % 2
@@ -357,24 +372,11 @@
         col_copies.append(
             share("col", me_c, cols, col_in.at[me_c, h], s_col, r_col, h * (cols - 1))
         )
+        if h == 0:
+            carry_copies = share("col", me_c, cols, carry_in.at[me_c], s_carry, r_carry)
 
     for copy in late_loads:
         copy.wait()
-    turned_hi, turned_lo = split(residual_ref[...].T)
-    tops = [slice(256 * unit, 256 * unit + 256) for unit in range(2)]
-    for unit in range(2):
-        multiply(
-            sums[2 * unit],
-            unit,
-            (row_sines_ref[0], row_sines_ref[1]),
-            (turned_hi[tops[unit]], turned_lo[tops[unit]]),
-        )
-    modal = jnp.concatenate([pltpu.matmul_pop(sums[2 * unit]) for unit in range(2)], axis=0)
-    phi, side_gain = decay(row_eigen_ref[...] + shift)
-    fill_decays(phi, slice(0, extent), side_down, side_up)
-    carry_in[me_c, 0:1, :] = jnp.sum(modal * side_down[...], axis=0, keepdims=True)
-    carry_in[me_c, 1:2, :] = jnp.sum(modal * side_up[...], axis=0, keepdims=True)
-    carry_copies = share("col", me_c, cols, carry_in.at[me_c], s_carry, r_carry)
 
     def across(value):
         high, low = split(value)

time: 20.1 us -> 20 us (level)
  no operation moved by 1% of the time
where the time goes in v6:
time: 20 us; the launch traced here: 19.8 us
  Pallas kernels  17.6 us (88%)
  between operations  2 us (10%)
    pallas_call x1, Pallas kernels, body(): pl.pallas_call(functools.partial(kernel, rows, cols, ready), out_shape=(j...  16.7 us
    pallas_call x1, Pallas kernels, body(): pl.pallas_call(update, out_shape=(jax.ShapeDtypeStruct((extent, width), f...  0.95 us

profile of v6, /device:TPU:0, one launch (start us, length us, event | category | flops | bytes accessed | tf_op | source)
XLA Modules:
  0.0 19.8 jit_solution(8656165112191274855)
XLA Ops:
  0.6 0.0 copy-start
  2.0 0.1 maximum_bitcast_fusion
  2.1 0.1 broadcast_in_dim.8.refs_7_
  2.1 16.7 %shard_map.113 = (f32[256,512]{1,0:T(8,128)S(1)}, f32[1,128]{1,0:T(1,128)S(1)}) custom-call(f32[256,512]{1,0:T(8,128)} %refs_0_.1, f32[16,128]{1,0:T(8,128)} %constant.12.clone.refs_1_, f32[1,256]{1,0:T(1,128)} %constant.13.clone.refs_2_, f32[512,256]{1,0:T(8,128)} %constant.14.clone.refs_3_, bf16[2,256,256]{2,1,0:T(8,128)(2,1)} %constant.15.clone.refs_4_, ...), custom_call_target="tpu_custom_call" | custom-call | tf_op jit(solution)/shard_map/pallas_call | solution.py:539
  18.8 0.0 copy-done
  18.8 0.9 %shard_map.114 = (f32[256,512]{1,0:T(8,128)}, f32[1]{0:T(128)}) custom-call(f32[256,512]{1,0:T(8,128)S(1)} %get-tuple-element.4.solved_ref, f32[256,512]{1,0:T(8,128)S(1)} %copy-done, f32[1,128]{1,0:T(1,128)S(1)} %get-tuple-element.5.ratio_in), custom_call_target="tpu_custom_call" | custom-call | tf_op jit(solution)/shard_map/pallas_call | solution.py:554
Async XLA Ops:
  0.6 18.2 %copy-start = (f32[256,512]{1,0:T(8,128)S(1)}, f32[256,512]{1,0:T(8,128)}, u32[]{:S(2)}) copy-start(f32[256,512]{1,0:T(8,128)} %direction_ref.1) | copy-start | bytes 1572868

commit v7 on v6

--- a/solution.py
+++ b/solution.py
@@ -193,9 +193,9 @@
     sources = 1 if ready else 2
     residual_hbm, waves_hbm, row_eigen_hbm, both_hbm, row_sines_hbm, col_sines_hbm = refs[:6]
     source_hbms = refs[6 : 6 + sources]
-    scalars_ref, out_ref, ratio_ref = refs[6 + sources : 9 + sources]
+    shift_ref, previous_ref, out_ref, ratio_ref = refs[6 + sources : 10 + sources]
     residual_ref, waves_ref, row_eigen_ref, both_ref, row_sines_ref, col_sines_ref = refs[
-        9 + sources : 15 + sources
+        10 + sources : 16 + sources
     ]
     (
         load_sems,
@@ -222,7 +222,7 @@
         s_block,
         r_block,
         *spare,
-    ) = refs[15 + sources :]
+    ) = refs[16 + sources :]
     me_r = lax.axis_index("row")
     me_c = lax.axis_index("col")
     extent, width = residual_ref.shape
@@ -287,7 +287,7 @@
             copies.append(copy)
         return copies
 
-    shift = scalars_ref[0:1, 0:1]
+    shift = shift_ref[0]
     waves_load.wait()
     theta, gain = decay(waves_ref[...] + shift)
     theta_ref[...] = theta
@@ -462,7 +462,7 @@
                 inner = jnp.sum(inner, axis=0, keepdims=True)
                 for k in range(rows):
                     inner = inner + quad_in[k]
-                ratio = jnp.sum(inner, axis=1, keepdims=True) / scalars_ref[1:2, 0:1]
+                ratio = jnp.sum(inner, axis=1, keepdims=True) / previous_ref[0]
                 ratio_ref[...] = jnp.broadcast_to(ratio, ratio_ref.shape)
             t = first // 128
             a_row = jnp.concatenate([amp_ref[0, t + i : t + i + 1, :] for i in range(2)], axis=1)
@@ -496,7 +496,6 @@
     dma = pltpu.SemaphoreType.DMA
     per_row, per_col = max(rows - 1, 1), max(cols - 1, 1)
     operands = (residual, *constants)
-    scalars = jnp.broadcast_to(jnp.stack([ground_shift, previous]), (2, 128))
     tiles = length // 128
     part = tiles // PARTS
     scratch = [pltpu.VMEM(x.shape, x.dtype) for x in operands[:6]] + [
@@ -542,7 +541,7 @@
             jax.ShapeDtypeStruct((extent, width), f32),
             jax.ShapeDtypeStruct((1, 128), f32),
         ),
-        in_specs=[hbm] * len(operands) + [vmem],
+        in_specs=[hbm] * len(operands) + [smem, smem],
         out_specs=(vmem, vmem),
         scratch_shapes=scratch,
         compiler_params=pltpu.CompilerParams(
@@ -550,7 +549,7 @@
             has_side_effects=True,
             vmem_limit_bytes=min(held + (held >> 2) + (8 << 20), 61 << 20),
         ),
-    )(*(pltpu.with_memory_space_constraint(x, pltpu.HBM) for x in operands), scalars)
+    )(*(pltpu.with_memory_space_constraint(x, pltpu.HBM) for x in operands), ground_shift, previous)
     return pl.pallas_call(
         update,
         out_shape=(

time: 20 us -> 20 us (level)
  no operation moved by 1% of the time
where the time goes in v7:
time: 20 us; the launch traced here: 19.7 us
  Pallas kernels  17.7 us (88%)
  between operations  2 us (10%)
    pallas_call x1, Pallas kernels, body(): pl.pallas_call(functools.partial(kernel, rows, cols, ready), out_shape=(j...  16.8 us
    pallas_call x1, Pallas kernels, body(): pl.pallas_call(update, out_shape=(jax.ShapeDtypeStruct((extent, width), f...  0.95 us

profile of v7, /device:TPU:0, one launch (start us, length us, event | category | flops | bytes accessed | tf_op | source)
XLA Modules:
  0.0 19.7 jit_solution(12384682425823148437)
XLA Ops:
  0.6 0.0 copy-start
  2.0 16.8 %shard_map.113 = (f32[256,512]{1,0:T(8,128)S(1)}, f32[1,128]{1,0:T(1,128)S(1)}) custom-call(f32[256,512]{1,0:T(8,128)} %refs_0_.1, f32[16,128]{1,0:T(8,128)} %constant.12.clone.refs_1_, f32[1,256]{1,0:T(1,128)} %constant.13.clone.refs_2_, f32[512,256]{1,0:T(8,128)} %constant.14.clone.refs_3_, bf16[2,256,256]{2,1,0:T(8,128)(2,1)} %constant.15.clone.refs_4_, ...), custom_call_target="tpu_custom_call" | custom-call | tf_op jit(solution)/shard_map/pallas_call | solution.py:538
  18.8 0.0 copy-done
  18.8 0.9 %shard_map.114 = (f32[256,512]{1,0:T(8,128)}, f32[1]{0:T(128)}) custom-call(f32[256,512]{1,0:T(8,128)S(1)} %get-tuple-element.4.solved_ref, f32[256,512]{1,0:T(8,128)S(1)} %copy-done, f32[1,128]{1,0:T(1,128)S(1)} %get-tuple-element.5.ratio_in), custom_call_target="tpu_custom_call" | custom-call | tf_op jit(solution)/shard_map/pallas_call | solution.py:553
Async XLA Ops:
  0.6 18.1 %copy-start = (f32[256,512]{1,0:T(8,128)S(1)}, f32[256,512]{1,0:T(8,128)}, u32[]{:S(2)}) copy-start(f32[256,512]{1,0:T(8,128)} %direction_ref.1) | copy-start | bytes 1572868
